TPU v7x, 256 devices: a whole 4x4x8 slice. The times are simulated.
256 devices in a mesh: rep: 2 (over core), dp: 128 (over x, y, z).
Axes of the slice: x: 4, y: 4, z: 8, core: 2. Of those that a mesh axis runs over, the one named last changes fastest.
Arguments:
- g_w_gate: bfloat16 [256, 2, 512, 1408], P(('rep', 'dp')), parts along dimension 0
- g_w_up: bfloat16 [256, 2, 512, 1408], P(('rep', 'dp')), parts along dimension 0
- g_w_down: bfloat16 [256, 2, 1408, 512], P(('rep', 'dp')), parts along dimension 0
- w_gate: bfloat16 [2, 512, 1408], replicated
- w_up: bfloat16 [2, 512, 1408], replicated
- w_down: bfloat16 [2, 1408, 512], replicated
- m_w_gate: float32 [2, 512, 1408], P(None, 'dp')
- m_w_up: float32 [2, 512, 1408], P(None, 'dp')
- m_w_down: float32 [2, 1408, 512], P(None, 'dp')
- v_w_gate: float32 [2, 512, 1408], P(None, 'dp')
- v_w_up: float32 [2, 512, 1408], P(None, 'dp')
- v_w_down: float32 [2, 1408, 512], P(None, 'dp')
Outputs:
- output 1: bfloat16 [4, 512, 1408], P('rep'), parts along dimension 0
- output 2: bfloat16 [4, 512, 1408], P('rep'), parts along dimension 0
- output 3: bfloat16 [4, 1408, 512], P('rep'), parts along dimension 0
- output 4: float32 [4, 512, 1408], P('rep', 'dp'), parts along dimension 0
- output 5: float32 [4, 512, 1408], P('rep', 'dp'), parts along dimension 0
- output 6: float32 [4, 1408, 512], P('rep', 'dp'), parts along dimension 0
- output 7: float32 [4, 512, 1408], P('rep', 'dp'), parts along dimension 0
- output 8: float32 [4, 512, 1408], P('rep', 'dp'), parts along dimension 0
- output 9: float32 [4, 1408, 512], P('rep', 'dp'), parts along dimension 0
There are 2 independent parts. A program takes and returns all parts, laid end to end along the dimension named above; an argument that names none is the same for every part.
All inputs are finite; a program needn't handle non-finite values.
Results may differ from a plain program's by a relative error of at most 0.022.
Values are sent between devices in bfloat16 or wider.
A program may use at most 768 MiB of HBM per device.

v0:
```python
import jax
import jax.numpy as jnp
from jax import lax
from jax.sharding import PartitionSpec as P


def adamw(w, m, v, g):
    m = 0.9 * m + 0.1 * g
    v = 0.95 * v + 0.05 * g * g
    step = m * lax.rsqrt(v + 1e-8) + 0.1 * w
    return (w - 0.02 * step).astype(jnp.bfloat16), m, v


def clipped(gradients, sum_of_squares, count):
    factor = jnp.minimum(1.0, 0.5 * lax.rsqrt(sum_of_squares / count + 1e-30))
    return [g * factor for g in gradients]


def solution(mesh):
    def step(*arrays):
        terms, weights, m, v = (arrays[i : i + 3] for i in (0, 3, 6, 9))
        gradients = [lax.psum_scatter(t[0], "dp", scatter_dimension=1, tiled=True).astype(jnp.float32) for t in terms]
        squares = lax.psum(sum(jnp.sum(g * g) for g in gradients), "dp")
        gradients = clipped(gradients, squares, lax.psum(1, "dp") * sum(g.size for g in gradients))
        me = lax.axis_index("dp")
        own = [lax.dynamic_slice_in_dim(w, me * one.shape[1], one.shape[1], 1).astype(jnp.float32) for w, one in zip(weights, m, strict=True)]
        new = [adamw(w, m, v, g) for w, m, v, g in zip(own, m, v, gradients, strict=True)]
        whole = [lax.all_gather(one[0], "dp", axis=1, tiled=True) for one in new]
        return (*whole, *(one[1] for one in new), *(one[2] for one in new))

    all_of, cut = P(None, None, None), P(None, "dp", None)
    return jax.shard_map(
        step,
        mesh=mesh,
        in_specs=(P(("rep", "dp"), None, None, None),) * 3 + (all_of,) * 3 + (cut,) * 6,
        out_specs=(P("rep", None, None),) * 3 + (P("rep", "dp", None),) * 6,
        check_vma=False,
    )
```

profile of v0, /device:TPU:2, one launch (start us, length us, event | category | flops | bytes accessed | tf_op | source)
XLA Modules:
  0.0 1003.1 jit_solution(16006152107737873505)
XLA Ops:
  7.2 0.0 all-reduce.6.cloned.1.call-start
  7.2 22.1 %copy.38 = bf16[1,2,1408,512]{3,1,2,0:T(2,128)(2,1)} copy(bf16[1,2,1408,512]{3,2,1,0:T(8,128)(2,1)} %param.14) | data formatting | bytes 5767168 | tf_op args[2]
  29.4 0.0 all-reduce.6.cloned.1.call-update
  29.4 0.0 all-gather.6.cloned.1.call-start
  29.5 0.5 copy-done.7
  30.0 0.6 dynamic-slice
  31.9 265.0 %all-reduce.6.cloned.1.call-done = (bf16[2,512,1408]{2,1,0:T(8,128)(2,1)}, bf16[2,512,1408]{2,1,0:T(8,128)(2,1)}, bf16[2,1408,512]{2,0,1:T(2,128)(2,1)}) async-done(((bf16[2,512,1408]{2,1,0:T(8,128)(2,1)}, bf16[2,512,1408]{2,1,0:T(8,128)(2,1)}, bf16[2,1408,512]{2,0,1:T(2,128)(2,1)}), (bf16[2,512,1408]{2,1,0:T(8,128)(2,1)}, bf16[2,512,1408]{2,1,0:T(8,128)(2,1)}, ...) | async-done | bytes 8650768
  296.9 1.5 fusion.9
  299.6 1.4 fusion.11
  301.7 307.4 %psum.7 = f32[]{:T(128)} all-reduce(f32[]{:T(128)S(6)} %add.65), channel_id=1, replica_groups=mesh['rep'=2,'dp'=128] {'dp'}, use_global_device_ids=true, to_apply=%region_6.0 | all-reduce | flops 1 | bytes 8 | tf_op jit(solution)/shard_map/psum | solution.py:23
  609.8 1.5 fusion.14
  611.3 0.6 copy.26
  612.0 0.0 all-gather.4.cloned.1.call-start
  612.1 1.5 fusion.8
  613.6 0.6 copy.25
  614.2 0.0 all-gather.8.cloned.1.call-start
  614.3 1.5 fusion.20
  615.8 0.0 all-gather.8.cloned.1.call-update
  615.9 143.5 %all-gather.6.cloned.1.call-done = bf16[2,512,1408]{2,0,1:T(2,128)(2,1)} async-done(((bf16[2,4,1408]{2,0,1:T(2,128)(2,1)}), bf16[2,512,1408]{2,0,1:T(2,128)(2,1)}) %all-gather.6.cloned.1.call-update) | async-done | bytes 2883600 | tf_op jit(solution)/shard_map/all_gather | solution.py:28
  759.4 3.7 copy.29
  763.1 113.3 %all-gather.4.cloned.1.call-done = bf16[2,512,1408]{2,0,1:T(2,128)(2,1)} async-done(((bf16[2,4,1408]{2,0,1:T(2,128)(2,1)}), bf16[2,512,1408]{2,0,1:T(2,128)(2,1)}) %all-gather.4.cloned.1.call-update) | async-done | bytes 2883600 | tf_op jit(solution)/shard_map/all_gather | solution.py:28
  876.4 3.7 copy.28
  880.1 112.6 %all-gather.8.cloned.1.call-done = bf16[2,1408,512]{2,0,1:T(2,128)(2,1)} async-done(((bf16[2,11,512]{2,0,1:T(2,128)(2,1)}), bf16[2,1408,512]{2,0,1:T(2,128)(2,1)}) %all-gather.8.cloned.1.call-update) | async-done | bytes 2883600 | tf_op jit(solution)/shard_map/all_gather | solution.py:28
  992.7 3.9 copy.30
  (18 shorter events, 0.1 us)
Async XLA Ops:
  7.2 607.1 %copy-start = (bf16[2,1408,512]{2,1,0:T(8,128)(2,1)S(1)}, bf16[2,1408,512]{2,1,0:T(8,128)(2,1)}, u32[]{:S(2)}) copy-start(bf16[2,1408,512]{2,1,0:T(8,128)(2,1)} %param.17) | copy-start | bytes 8650756
  7.2 289.7 %all-reduce.6.cloned.1.call-start = ((), (), s32[]{:S(2)}) async-start(), calls=%async_computation.3 | async-start | bytes 17301504
  29.4 0.7 copy-start.7
  29.4 580.5 %copy-start.3 = (f32[2,4,1408]{2,1,0:T(4,128)S(1)}, f32[2,4,1408]{2,1,0:T(4,128)}, u32[]{:S(2)}) copy-start(f32[2,4,1408]{2,1,0:T(4,128)} %param.22) | copy-start | bytes 135172
  29.4 580.5 %copy-start.4 = (f32[2,4,1408]{2,1,0:T(4,128)S(1)}, f32[2,4,1408]{2,1,0:T(4,128)}, u32[]{:S(2)}) copy-start(f32[2,4,1408]{2,1,0:T(4,128)} %param.19) | copy-start | bytes 135172
  29.4 582.7 %copy-start.5 = (f32[2,4,1408]{2,1,0:T(4,128)S(1)}, f32[2,4,1408]{2,1,0:T(4,128)}, u32[]{:S(2)}) copy-start(f32[2,4,1408]{2,1,0:T(4,128)} %param.21) | copy-start | bytes 135172
  29.4 582.7 %copy-start.6 = (f32[2,4,1408]{2,1,0:T(4,128)S(1)}, f32[2,4,1408]{2,1,0:T(4,128)}, u32[]{:S(2)}) copy-start(f32[2,4,1408]{2,1,0:T(4,128)} %param.18) | copy-start | bytes 135172
  29.4 584.9 %copy-start.1 = (f32[2,11,512]{2,0,1:T(2,128)S(1)}, f32[2,11,512]{2,0,1:T(2,128)}, u32[]{:S(2)}) copy-start(f32[2,11,512]{2,0,1:T(2,128)} %param.23) | copy-start | bytes 135172
  29.4 584.9 %copy-start.2 = (f32[2,11,512]{2,0,1:T(2,128)S(1)}, f32[2,11,512]{2,0,1:T(2,128)}, u32[]{:S(2)}) copy-start(f32[2,11,512]{2,0,1:T(2,128)} %param.20) | copy-start | bytes 135172
  29.4 729.9 %all-gather.6.cloned.1.call-start = ((), (), s32[]{:S(2)}) async-start(), calls=%async_computation.1 | async-start | bytes 2906112 | tf_op jit(solution)/shard_map/all_gather | solution.py:28
  612.0 264.4 %all-gather.4.cloned.1.call-start = ((), (), s32[]{:S(2)}) async-start(), calls=%async_computation | async-start | bytes 2906112 | tf_op jit(solution)/shard_map/all_gather | solution.py:28
  614.2 378.5 %all-gather.8.cloned.1.call-start = ((), (), s32[]{:S(2)}) async-start(), calls=%async_computation.2 | async-start | bytes 2906112 | tf_op jit(solution)/shard_map/all_gather | solution.py:28
Sparse Core Ops, SparseCore 0:
  29.6 267.2 all-reduce.5
  612.1 147.1 all-gather.5
  763.6 112.7 all-gather.3
  879.9 112.7 all-gather.7
where the time goes:
time: 1000 us
  waiting for transfers between devices  634 us (63%)
  blocking collectives  307 us (31%)
  local copies, waits for them, and re-layouts  35.9 us (4%)
  between operations  17.8 us (2%)
    all_gather x3, waiting for transfers between devices, step(): whole = [lax.all_gather(one[0], 'dp', axis=1, tiled=True) for one in new]  369 us
    psum x1, blocking collectives, step(): squares = lax.psum(sum((jnp.sum(g * g) for g in gradients)), 'dp')  307 us
    unnamed x5, waiting for transfers between devices  265 us
    unnamed x21, local copies, waits for them, and re-layouts  34.6 us
  transfers between devices with their start and end apart: 4, of which 4 were waited for; matrix products, arithmetic and copies ran while one was open for 1% of the time, Pallas kernels for 0%

commit v1 on v0

v1 whole, which is shorter than its diff:
```python
import functools

import jax
import jax.numpy as jnp
from jax import lax
from jax.experimental import pallas as pl
from jax.experimental.pallas import tpu as pltpu
from jax.sharding import PartitionSpec as P

X, Y, Z = 4, 4, 8
F = 1408
COUNT = 3 * 2 * 512 * F
SEMS = 256
LOADS = 32
f32, bf16 = jnp.float32, jnp.bfloat16
BOTH = (0, 1)
WAYS = (1, -1)
LONG = ((0, 1), (1, -1))
SHORT = ((1, 1), (0, -1))


def chains(n):
    return [(*one, n // 2) for one in LONG] + [(*one, n // 2 - 1) for one in SHORT]


def slots(n):
    return {key: i for i, key in enumerate((h, s, t) for h, s, length in chains(n) for t in range(1, length + 1))}


def sixteen(i):
    return pl.ds(pl.multiple_of(i * 16, 16), 16)


def loop(n, body):
    def step(i, carry):
        body(i)
        return carry

    lax.fori_loop(0, n, step, 0)


def kernel(gg, gu, gd, wg, wu, wd, mg, mu, md, vg, vu, vd, *rest):
    (og, ou, od, omg, omu, omd, ovg, ovu, ovd) = rest[:9]
    (G, GD, L1, F1, B1, L2, F2, ZS, ZF, ZL, LZ, FD, BD, LDX, DS, YS, YF, YL, NS, NL, WG, WD, WZ, YW, ssem, rsem, lsem, osem) = rest[9:]
    d = lax.axis_index("dp")
    x, y, z = d // 32, (d // 8) % 4, d % 8
    place = {"x": (x, 4), "y": (y, 4), "z": (z, 8)}

    def at(axis, k):
        p, n = place[axis]
        return lax.rem(p + (k + n) % n, n)

    def device(axis, k):
        p = at(axis, k)
        return {"dp": {"x": p * 32 + y * 8 + z, "y": x * 32 + p * 8 + z, "z": x * 32 + y * 8 + p}[axis]}

    used = [0]
    pending = []

    def send(src, dst, axis, k):
        i = used[0]
        used[0] += 1
        copy = pltpu.make_async_remote_copy(
            src_ref=src, dst_ref=dst, send_sem=ssem.at[i], recv_sem=rsem.at[i],
            device_id=device(axis, k), device_id_type=pl.DeviceIdType.MESH,
        )
        copy.start()
        pending.append(copy)
        return copy

    loads = {}

    def load(key, src, dst):
        copy = pltpu.make_async_copy(src, dst, lsem.at[len(loads)])
        copy.start()
        loads[key] = copy

    stores = []

    def store(src, dst):
        copy = pltpu.make_async_copy(src, dst, osem.at[len(stores)])
        copy.start()
        stores.append(copy)

    class Scatter:
        def __init__(self, axis, own, landing, add, need=None):
            self.axis, self.own, self.landing, self.add, self.need = axis, own, landing, add, need
            self.n = place[axis][1]
            self.length = {(h, s): length for h, s, length in chains(self.n)}
            self.slot = slots(self.n)
            self.copies = {}

        def at(self, h, s, t):
            return self.landing.at[self.slot[h, s, t]]

        def first(self, h, s):
            k = s * self.length[h, s]
            if self.need:
                self.need(h, k)
            self.copies[h, s, 1] = send(self.own(h, k), self.at(h, s, 1), self.axis, s)

        def start(self):
            for h, s, _ in chains(self.n):
                self.first(h, s)

        def arrive(self, h, s, t):
            self.copies[h, s, t].wait_recv()
            if t < self.length[h, s]:
                k = s * (self.length[h, s] - t)
                if self.need:
                    self.need(h, k)
                self.add(self.at(h, s, t), h, k)
                self.copies[h, s, t + 1] = send(self.at(h, s, t), self.at(h, s, t + 1), self.axis, s)

        def last(self, h):
            for s in WAYS:
                self.arrive(h, s, self.length[h, s])
            return [self.at(h, s, self.length[h, s]) for s in WAYS]

    class Gather:
        def __init__(self, axis, part):
            self.axis, self.part = axis, part
            self.n = place[axis][1]
            self.length = {(h, s): length for h, s, length in chains(self.n)}
            self.copies = {}

        def push(self, h, s, t):
            ref = self.part(h, -s * (t - 1))
            self.copies[h, s, t] = send(ref, ref, self.axis, s)

        def start(self):
            for h, s, _ in chains(self.n):
                self.push(h, s, 1)

        def arrive(self, h, s, t):
            self.copies[h, s, t].wait_recv()
            if t < self.length[h, s]:
                self.push(h, s, t + 1)
            return -s * t

    def load_wide(f, h, k):
        if f == 0:
            load((f, h, k), (gg, gu)[h].at[0, at("x", k)], G.at[h, 0, at("x", k)])
        else:
            load((f, h, k), (gg, gu)[h].at[1, :, at("y", k)], G.at[h, 1, :, at("y", k)])

    def load_down(h, k):
        load((2, h, k % 8), gd.at[h, at("z", k)], GD.at[h, at("z", k)])

    for f in BOTH:
        for h in BOTH:
            load_wide(f, h, 2)
    for h in BOTH:
        load_down(h, 4)
    for f in BOTH:
        for h, k in ((1, 1), (0, 3)):
            load_wide(f, h, k)
    for h, k in ((1, 3), (0, 5), (0, 3), (1, 5), (1, 2), (0, 6), (0, 2), (1, 6)):
        load_down(h, k)
    for f in BOTH:
        for h, k in ((0, 1), (1, 3)):
            load_wide(f, h, k)
    for h, k in ((0, 1), (1, 7), (1, 1), (0, 7)):
        load_down(h, k)
    for f in BOTH:
        for h in BOTH:
            load_wide(f, h, 0)
    for h in BOTH:
        load_down(h, 0)
    ready = set()

    def need(f, n):
        def wait(h, k):
            key = (f, h, k % n)
            if key not in ready:
                ready.add(key)
                loads[key].wait()

        return wait

    partners = [(a, k) for a, n in (("x", 4), ("y", 4), ("z", 8)) for k in range(1, n)]
    barrier = pltpu.get_barrier_semaphore()
    for a, k in partners:
        pl.semaphore_signal(barrier, inc=1, device_id=device(a, k), device_id_type=pl.DeviceIdType.MESH)
    pl.semaphore_wait(barrier, len(partners))

    def wide(f):
        def own(h, k):
            return G.at[h, 0, at("x", k)] if f == 0 else G.at[h, 1, :, at("y", k)]

        return own

    def add_wide(f):
        def add(got, h, k):
            own = wide(f)(h, k)

            def body(i):
                rows = (i // 2, sixteen(i % 2))
                got[rows] = (got[rows].astype(f32) + own[rows].astype(f32)).astype(bf16)

            loop(8, body)

        return add

    def add_down(got, h, k):
        own = GD.at[h, at("z", k)]

        def body(i):
            got[i] = (got[i].astype(f32) + own[i].astype(f32)).astype(bf16)

        loop(4, body)

    first = [Scatter("xy"[f], wide(f), L1.at[f], add_wide(f), need(f, 4)) for f in BOTH]
    down = Scatter("z", lambda h, k: GD.at[h, at("z", k)], LZ, add_down, need(2, 8))

    def end_wide(f, h):
        a, b = first[f].last(h)
        need(f, 4)(h, 0)
        own = wide(f)(h, 0)

        def body(i):
            rows = (i // 2, sixteen(i % 2))
            total = own[rows].astype(f32) + a[rows].astype(f32) + b[rows].astype(f32)
            F1[(f, h, *rows)] = total
            B1[(f, h, *rows)] = total.astype(bf16)

        loop(8, body)

    def end_down(h):
        a, b = down.last(h)
        need(2, 8)(h, 0)
        own = GD.at[h, at("z", 0)]

        def body(i):
            total = own[i].astype(f32) + a[i].astype(f32) + b[i].astype(f32)
            FD[h, i] = total
            BD[h, i] = total.astype(bf16)

        loop(4, body)

    def add_second(f):
        axis = "yx"[f]

        def add(got, h, k):
            own = F1.at[f, h, at(axis, k)]

            def body(i):
                rows = (sixteen(i),)
                got[rows] = (got[rows].astype(f32) + own[rows]).astype(bf16)

            loop(2, body)

        return add

    def second_own(f):
        axis = "yx"[f]
        return lambda h, k: B1.at[f, h, at(axis, k)]

    def add_down_second(got, h, k):
        got[...] = (got[...].astype(f32) + FD[h, at("x", k)]).astype(bf16)

    second = [Scatter("yx"[f], second_own(f), L2.at[f], add_second(f)) for f in BOTH]
    down_second = Scatter("x", lambda h, k: BD.at[h, at("x", k)], LDX, add_down_second)

    def end_second(f, h):
        a, b = second[f].last(h)
        own = F1.at[f, h, at("yx"[f], 0)]

        def body(i):
            rows = (sixteen(i),)
            F2[(f, h, *rows)] = own[rows] + a[rows].astype(f32) + b[rows].astype(f32)

        loop(2, body)

    def arrive_pair(ring, t, short=False):
        for h, s in SHORT if short else LONG:
            ring.arrive(h, s, t)

    for f in BOTH:
        for h, s in LONG:
            first[f].first(h, s)
    for h, s in LONG:
        down.first(h, s)
    for f in BOTH:
        for h, s in SHORT:
            first[f].first(h, s)
    for h, s in SHORT:
        down.first(h, s)
    arrive_pair(down, 1)
    arrive_pair(down, 1, True)
    arrive_pair(first[0], 1)
    arrive_pair(first[1], 1)
    arrive_pair(down, 2)
    arrive_pair(down, 2, True)
    arrive_pair(down, 3)
    for f in BOTH:
        for h in BOTH:
            end_wide(f, h)
        second[f].start()
    for h in BOTH:
        end_down(h)
    down_second.start()
    for f in BOTH:
        arrive_pair(second[f], 1)
    arrive_pair(down_second, 1)
    for f in BOTH:
        for h in BOTH:
            end_second(f, h)

    for h in BOTH:
        for j in range(4):
            t0, t1 = (F2[f, h, 8 * j : 8 * j + 8, :] for f in BOTH)
            for i, block in enumerate((jnp.concatenate([t0[:4], t1[:4]], 0), jnp.concatenate([t0[4:], t1[4:]], 0))):
                ZF[2 * j + i, h] = block
                ZS[2 * j + i, h] = block.astype(bf16)
    far = (4, 3, 5, 2, 6, 1, 7)
    third = {k: send(ZS.at[at("z", k)], ZL.at[k], "z", k) for k in far}

    for h in BOTH:
        a, b = down_second.last(h)
        DS[h, :88] = FD[h, at("x", 0)] + a[...].astype(f32) + b[...].astype(f32)
        DS[h, 88:] = jnp.zeros((8, 256), f32)
        for j in range(4):
            block = DS[h, 22 * j : 22 * j + 24, :]
            YF[j, h] = block
            YS[j, h] = block.astype(bf16)
    third_down = {k: send(YS.at[at("y", k)], YL.at[k], "y", k) for k in (2, 1, 3)}

    for k in (1, 3, 2):
        third_down[k].wait_recv()
    real = lax.broadcasted_iota(jnp.int32, (24, 256), 0) < 22
    squares = jnp.zeros((), f32)
    g_down = []
    for h in BOTH:
        total = YF[y, h]
        for k in (1, 2, 3):
            total = total + YL[k, h].astype(f32)
        total = jnp.where(real, total, 0.0).astype(bf16).astype(f32)
        g_down.append(total)
        squares += jnp.sum(total * total)
    for k in reversed(far):
        third[k].wait_recv()
    g_wide = []
    for h in BOTH:
        total = ZF[z, h]
        for k in range(1, 8):
            total = total + ZL[k, h].astype(f32)
        total = total.astype(bf16).astype(f32)
        g_wide.append(total)
        squares += jnp.sum(total * total)

    total = jnp.full((8, 128), squares, f32)
    for i, (a, n) in enumerate((("x", 4), ("y", 4), ("z", 8))):
        NS[i] = total
        copies = [send(NS.at[i], NL.at[i, k], a, k) for k in range(1, n)]
        for copy in copies:
            copy.wait_recv()
        for k in range(1, n):
            total = total + NL[i, k]
    factor = jnp.minimum(1.0, 0.5 * lax.rsqrt(total / COUNT + 1e-30))[0:1, 0:1]

    def adamw(w, m, v, g):
        m = 0.9 * m + 0.1 * g
        v = 0.95 * v + 0.05 * g * g
        return (w - 0.02 * (m * lax.rsqrt(v + 1e-8) + 0.1 * w)).astype(bf16), m, v

    for h, (w_, m_, v_, om, ov) in enumerate(((wg, mg, vg, omg, ovg), (wu, mu, vu, omu, ovu))):
        w, m, v = (jnp.concatenate([r[0].astype(f32), r[1].astype(f32)], 0) for r in (w_, m_, v_))
        w, m, v = adamw(w, m, v, g_wide[h] * factor)
        WZ[z, h] = w
        for layer in BOTH:
            om[layer] = m[4 * layer : 4 * layer + 4]
            ov[layer] = v[4 * layer : 4 * layer + 4]
    g = jnp.concatenate(g_down, 1) * factor
    for h in BOTH:
        DS[h, :24] = jnp.zeros((24, 256), f32)
    for layer in BOTH:
        w, m, v = adamw(wd[layer].astype(f32), md[layer], vd[layer], g[11 * layer : 11 * layer + 11])
        omd[layer], ovd[layer] = m, v
        for h in BOTH:
            DS[h, 11 * layer : 11 * layer + 11, :] = w[:, 256 * h : 256 * h + 256].astype(f32)
    for h in BOTH:
        YW[y, h] = DS[h, :24].astype(bf16)

    wide_z = {k: send(WZ.at[z], WZ.at[z], "z", k) for k in far}
    down_y = {k: send(YW.at[y], YW.at[y], "y", k) for k in (2, 1, 3)}
    for k in (1, 3, 2):
        down_y[k].wait_recv()
    for h in BOTH:
        for j in range(4):
            DS[h, 22 * j : 22 * j + 24, :] = YW[j, h].astype(f32)
        WD[h, z, x] = DS[h, :88].astype(bf16)
    down_x = Gather("x", lambda h, k: WD.at[h, z, at("x", k)])
    down_x.start()
    for k in reversed(far):
        wide_z[k].wait_recv()
    for h in BOTH:
        for layer in BOTH:
            rows = slice(4 * layer, 4 * layer + 4)
            for j in range(2):
                parts = [WZ[4 * j + i, h].astype(f32)[rows] for i in range(4)]
                WG[h, layer, x, y, 16 * j : 16 * j + 16, :] = jnp.concatenate(parts, 0).astype(bf16)
    near = [Gather("y", lambda h, k: WG.at[h, 0, x, at("y", k)]), Gather("x", lambda h, k: WG.at[h, 1, at("x", k), y])]
    for ring in near:
        ring.start()
    arrive_pair(down_x, 1)
    arrive_pair(down_x, 1, True)
    arrive_pair(down_x, 2)
    down_z = Gather("z", lambda h, k: WD.at[h, at("z", k)])
    down_z.start()

    def put_wide(f, h, k):
        out = (og, ou)[h]
        if f == 0:
            store(WG.at[h, 0, at("x", k)], out.at[0, at("x", k)])
        else:
            store(WG.at[h, 1, :, at("y", k)], out.at[1, :, at("y", k)])

    def put_down(h, k):
        store(WD.at[h, at("z", k)], od.at[h, at("z", k)])

    for ring in near:
        arrive_pair(ring, 1)
    for ring in near:
        arrive_pair(ring, 1, True)
    far_rings = [Gather("x", lambda h, k: WG.at[h, 0, at("x", k)]), Gather("y", lambda h, k: WG.at[h, 1, :, at("y", k)])]
    for f in BOTH:
        arrive_pair(near[f], 2)
        far_rings[f].start()
    for h in BOTH:
        put_down(h, 0)
        for f in BOTH:
            put_wide(f, h, 0)

    def down_arrive(t, short=False):
        for h, s in SHORT if short else LONG:
            put_down(h, down_z.arrive(h, s, t))

    def wide_arrive(t, short=False):
        for f in BOTH:
            for h, s in SHORT if short else LONG:
                put_wide(f, h, far_rings[f].arrive(h, s, t))

    down_arrive(1)
    down_arrive(1, True)
    down_arrive(2)
    wide_arrive(1)
    down_arrive(2, True)
    down_arrive(3)
    wide_arrive(1, True)
    down_arrive(3, True)
    down_arrive(4)
    wide_arrive(2)
    for copy in pending:
        copy.wait_send()
    for copy in stores:
        copy.wait()


def step_kernel(*args):
    hbm, vmem = pl.BlockSpec(memory_space=pl.ANY), pl.BlockSpec(memory_space=pltpu.VMEM)
    wide, deep = (2, 4, F), (2, 11, 512)
    unit, half = (4, 32, F), (4, 88, 256)
    pair, square, whole_down = (2, 2), (4, *unit), (2, 8, *half)
    blocks, small, tile = (8, 2, 8, F), (4, 2, 24, 256), (8, 128)
    shape = jax.ShapeDtypeStruct
    return pl.pallas_call(
        kernel,
        out_shape=(
            shape((2, *square), bf16), shape((2, *square), bf16), shape(whole_down, bf16),
            shape(wide, f32), shape(wide, f32), shape(deep, f32), shape(wide, f32), shape(wide, f32), shape(deep, f32),
        ),
        in_specs=[hbm] * 3 + [vmem] * 9,
        out_specs=(hbm,) * 3 + (vmem,) * 6,
        scratch_shapes=[
            pltpu.VMEM((*pair, *square), bf16),
            pltpu.VMEM(whole_down, bf16),
            pltpu.VMEM((2, 6, *unit), bf16),
            pltpu.VMEM((*pair, *unit), f32),
            pltpu.VMEM((*pair, *unit), bf16),
            pltpu.VMEM((2, 6, *unit[1:]), bf16),
            pltpu.VMEM((*pair, *unit[1:]), f32),
            pltpu.VMEM(blocks, bf16),
            pltpu.VMEM(blocks, f32),
            pltpu.VMEM(blocks, bf16),
            pltpu.VMEM((14, *half), bf16),
            pltpu.VMEM((2, *half), f32),
            pltpu.VMEM((2, *half), bf16),
            pltpu.VMEM((6, *half[1:]), bf16),
            pltpu.VMEM((2, 96, 256), f32),
            pltpu.VMEM(small, bf16),
            pltpu.VMEM(small, f32),
            pltpu.VMEM(small, bf16),
            pltpu.VMEM((3, *tile), f32),
            pltpu.VMEM((3, 8, *tile), f32),
            pltpu.VMEM((*pair, *square), bf16),
            pltpu.VMEM(whole_down, bf16),
            pltpu.VMEM(blocks, bf16),
            pltpu.VMEM(small, bf16),
            pltpu.SemaphoreType.DMA((SEMS,)),
            pltpu.SemaphoreType.DMA((SEMS,)),
            pltpu.SemaphoreType.DMA((LOADS,)),
            pltpu.SemaphoreType.DMA((LOADS,)),
        ],
        compiler_params=pltpu.CompilerParams(collective_id=0, has_side_effects=True, vmem_limit_bytes=60 * 2**20),
        name="clipped_step",
    )(*args)


def solution(mesh):
    def step(gg, gu, gd, wg, wu, wd, *moments):
        gg, gu = (g.reshape(2, 4, 4, 32, F) for g in (gg, gu))
        gd = gd.reshape(2, 4, 4, 8, 11, 2, 256).transpose(5, 3, 1, 2, 0, 4, 6).reshape(2, 8, 4, 88, 256)
        me = lax.axis_index("dp")
        own = [lax.dynamic_slice_in_dim(w, me * n, n, 1) for w, n in ((wg, 4), (wu, 4), (wd, 11))]
        og, ou, od, *rest = step_kernel(gg, gu, gd, *own, *moments)
        og, ou = (o.reshape(2, 512, F) for o in (og, ou))
        od = od.reshape(2, 8, 4, 4, 2, 11, 256).transpose(4, 2, 3, 1, 5, 0, 6).reshape(2, F, 512)
        return (og, ou, od, *rest)

    all_of, cut = P(None, None, None), P(None, "dp", None)
    return jax.shard_map(
        step,
        mesh=mesh,
        in_specs=(P(("rep", "dp"), None, None, None),) * 3 + (all_of,) * 3 + (cut,) * 6,
        out_specs=(P("rep", None, None),) * 3 + (P("rep", "dp", None),) * 6,
        check_vma=False,
    )
```

time: 1000 us -> 159 us (0.16)
  waiting for transfers between devices: 634 us -> 0 us
  blocking collectives: 307 us -> 0 us
  Pallas kernels: 0 us -> 113 us
  between operations: 17.8 us -> 0.7 us
    all_gather x3 -> x0, waiting for transfers between devices: 369 us -> none  [step(): whole = [lax.all_gather(one[0], 'dp', axis=1, tiled=True) for one in new]]
    psum x1 -> x0, blocking collectives: 307 us -> none  [step(): squares = lax.psum(sum((jnp.sum(g * g) for g in gradients)), 'dp')]
    unnamed x5 -> x0, waiting for transfers between devices: 265 us -> none
    pallas_call x0 -> x1, Pallas kernels: none -> 113 us  [step_kernel(): pl.pallas_call(kernel, out_shape=(shape((2, *square), bf16), shape((2, *s...]
    unnamed x21 -> x22, local copies, waits for them, and re-layouts: 34.6 us -> 15.5 us
    reshape x0 -> x3, local copies, waits for them, and re-layouts: none -> 16.6 us  [the longest x2 9.16 us: step(): gd.reshape(2, 4, 4, 8, 11, 2, 256).transpose(5, 3, 1, 2, 0, 4, 6)]
  transfers between devices with their start and end apart: 4 -> 0, of which waited for: 4 -> 0; matrix products, arithmetic and copies ran while one was open for 1% -> 0% of each run, Pallas kernels for 0% -> 0%
where the time goes in v1:
time: 159 us; the launch traced here: 158 us
  Pallas kernels  113 us (71%)
  local copies, waits for them, and re-layouts  44.4 us (28%)
    pallas_call x1, Pallas kernels, step_kernel(): pl.pallas_call(kernel, out_shape=(shape((2, *square), bf16), shape((2, *s...  113 us
    unnamed x22, local copies, waits for them, and re-layouts  15.5 us
    reshape x2, local copies, waits for them, and re-layouts, step(): gd.reshape(2, 4, 4, 8, 11, 2, 256).transpose(5, 3, 1, 2, 0, 4, 6)  9.16 us
    reshape x1, local copies, waits for them, and re-layouts, step(): od.reshape(2, 8, 4, 4, 2, 11, 256).transpose(4, 2, 3, 1, 5, 0, 6)  7.44 us
    transpose x1, local copies, waits for them, and re-layouts, step(): od.reshape(2, 8, 4, 4, 2, 11, 256).transpose(4, 2, 3, 1, 5, 0, 6)  4.54 us
    pallas_call x1, local copies, waits for them, and re-layouts, step_kernel(): pl.pallas_call(kernel, out_shape=(shape((2, *square), bf16), shape((2, *s...  3.44 us

profile of v1, /device:TPU:2, one launch (start us, length us, event | category | flops | bytes accessed | tf_op | source)
XLA Modules:
  0.0 158.1 jit_solution(16862648452772743897)
XLA Ops:
  0.6 0.0 copy-start
  0.7 1.8 %copy-done = bf16[2,1408,512]{2,1,0:T(8,128)(2,1)S(1)} copy-done((bf16[2,1408,512]{2,1,0:T(8,128)(2,1)S(1)}, bf16[2,1408,512]{2,1,0:T(8,128)(2,1)}, u32[]{:S(2)}) %copy-start) | copy-done | bytes 2883608
  2.5 0.6 constant_dynamic-slice_fusion.wd
  3.1 1.5 constant_dynamic-slice_fusion.1
  4.5 1.4 copy.35.md
  6.0 1.4 copy.36.vd
  7.4 6.9 %reshape.44 = bf16[2,4,4,8,11,2,256]{6,5,4,3,2,1,0:T(2,128)(2,1)} reshape(bf16[1,2,1408,512]{3,2,1,0:T(8,128)(2,1)} %param.14) | data formatting | bytes 5767168 | tf_op jit(solution)/shard_map/reshape | solution.py:513
  14.3 2.3 %copy.33 = bf16[2,8,4,4,2,11,256]{6,1,5,4,3,2,0:T(8,128)(2,1)S(1)} copy(bf16[2,8,4,4,2,11,256]{6,0,5,1,3,2,4:T(2,128)(2,1)} %bitcast.13) | data formatting | bytes 5767168 | tf_op jit(solution)/shard_map/transpose | solution.py:513
  16.6 2.2 %copy.34.gd = bf16[2,8,4,88,256]{4,3,2,1,0:T(8,128)(2,1)} copy(bf16[2,8,4,88,256]{4,1,3,2,0:T(8,128)(2,1)S(1)} %bitcast.11) | data formatting | bytes 5767168 | tf_op jit(solution)/shard_map/reshape | solution.py:513
  18.8 113.0 %clipped_step.1 = (bf16[2,4,4,32,1408]{4,3,2,1,0:T(8,128)(2,1)}, bf16[2,4,4,32,1408]{4,3,2,1,0:T(8,128)(2,1)}, bf16[2,8,4,88,256]{4,3,2,1,0:T(8,128)(2,1)}, f32[...) custom-call(bf16[2,4,4,32,1408]{4,3,2,1,0:T(8,128)(2,1)} %bitcast.14, ...), custom_call_target="tpu_custom_call" | custom-call | tf_op jit(solution)/shard_map/clipped_step/pallas_call | solution.py:467
  131.9 1.5 copy.39
  133.4 1.5 copy.40
  134.8 3.4 %copy.37 = bf16[2,8,4,88,256]{4,1,3,2,0:T(8,128)(2,1)S(1)} copy(bf16[2,8,4,88,256]{4,3,2,1,0:T(8,128)(2,1)} %get-tuple-element.20) | data formatting | bytes 5767168 | tf_op jit(solution)/shard_map/clipped_step/pallas_call | solution.py:467
  138.3 4.5 %copy.38 = bf16[2,4,4,8,11,2,256]{6,5,4,3,2,1,0:T(2,128)(2,1)} copy(bf16[2,4,4,8,11,2,256]{6,3,4,0,2,1,5:T(8,128)(2,1)S(1)} %bitcast.12) | data formatting | bytes 5767168 | tf_op jit(solution)/shard_map/transpose | solution.py:518
  142.8 7.4 %reshape.49 = bf16[2,1408,512]{2,1,0:T(8,128)(2,1)} reshape(bf16[2,4,4,8,11,2,256]{6,5,4,3,2,1,0:T(2,128)(2,1)} %copy.38) | data formatting | bytes 5767168 | tf_op jit(solution)/shard_map/reshape | solution.py:518
  150.3 3.8 %copy.47 = bf16[2,512,1408]{2,1,0:T(8,128)(2,1)} copy(bf16[2,512,1408]{2,1,0:T(8,128)(2,1)} %bitcast.17) | data formatting | bytes 5767168
  154.0 0.0 copy-done.1
  154.0 0.0 copy-start.2
  154.0 1.6 copy.48
  155.6 0.0 copy-done.5
  155.6 0.6 copy.49
  156.3 0.6 copy.50
  156.9 0.6 copy.51
  157.5 0.6 copy.52
  (7 shorter events, 0.0 us)
Async XLA Ops:
  0.6 1.8 %copy-start = (bf16[2,1408,512]{2,1,0:T(8,128)(2,1)S(1)}, bf16[2,1408,512]{2,1,0:T(8,128)(2,1)}, u32[]{:S(2)}) copy-start(bf16[2,1408,512]{2,1,0:T(8,128)(2,1)} %param.17) | copy-start | bytes 8650756
  150.3 3.8 %copy-start.1 = (bf16[2,4,4,32,1408]{4,3,2,1,0:T(8,128)(2,1)S(1)}, bf16[2,4,4,32,1408]{4,3,2,1,0:T(8,128)(2,1)}, u32[]{:S(2)}) copy-start(bf16[2,4,4,32,1408]{4,3,2,1,0:T(8,128)(2,1)} %get-tuple-element.19) | copy-start | bytes 8650756
  154.0 1.6 %copy-start.5 = (f32[2,4,1408]{2,1,0:T(4,128)S(1)}, f32[2,4,1408]{2,1,0:T(4,128)}, u32[]{:S(2)}) copy-start(f32[2,4,1408]{2,1,0:T(4,128)} %get-tuple-element.68) | copy-start | bytes 135172
  154.0 2.2 %copy-start.4 = (f32[2,4,1408]{2,1,0:T(4,128)S(1)}, f32[2,4,1408]{2,1,0:T(4,128)}, u32[]{:S(2)}) copy-start(f32[2,4,1408]{2,1,0:T(4,128)} %get-tuple-element.69) | copy-start | bytes 135172
  154.0 2.8 %copy-start.3 = (f32[2,4,1408]{2,1,0:T(4,128)S(1)}, f32[2,4,1408]{2,1,0:T(4,128)}, u32[]{:S(2)}) copy-start(f32[2,4,1408]{2,1,0:T(4,128)} %get-tuple-element.71) | copy-start | bytes 135172
  154.0 3.5 %copy-start.2 = (f32[2,4,1408]{2,1,0:T(4,128)S(1)}, f32[2,4,1408]{2,1,0:T(4,128)}, u32[]{:S(2)}) copy-start(f32[2,4,1408]{2,1,0:T(4,128)} %get-tuple-element.72) | copy-start | bytes 135172

commit v2 on v1

--- a/solution.py
+++ b/solution.py
@@ -12,6 +12,7 @@
 COUNT = 3 * 2 * 512 * F
 SEMS = 256
 LOADS = 32
+ROWS = 704
 f32, bf16 = jnp.float32, jnp.bfloat16
 BOTH = (0, 1)
 WAYS = (1, -1)
@@ -39,9 +40,9 @@
     lax.fori_loop(0, n, step, 0)
 
 
-def kernel(gg, gu, gd, wg, wu, wd, mg, mu, md, vg, vu, vd, *rest):
-    (og, ou, od, omg, omu, omd, ovg, ovu, ovd) = rest[:9]
-    (G, GD, L1, F1, B1, L2, F2, ZS, ZF, ZL, LZ, FD, BD, LDX, DS, YS, YF, YL, NS, NL, WG, WD, WZ, YW, ssem, rsem, lsem, osem) = rest[9:]
+def kernel(gg, gu, gd, wg, wu, wd, mg, mu, md, vg, vu, vd, WG, OD, gwide, gdown, *scratch):
+    (G, GR, GD, L1, F1, B1, L2, F2, ZS, ZF, ZL, LZ, FD, BD, LDX, DS, YS, YF, YL, NS, NL, WD, WZ, YW, PF, PB, OW, OWD) = scratch[:-4]
+    ssem, rsem, lsem, wsem = scratch[-4:]
     d = lax.axis_index("dp")
     x, y, z = d // 32, (d // 8) % 4, d % 8
     place = {"x": (x, 4), "y": (y, 4), "z": (z, 8)}
@@ -75,13 +76,6 @@
         copy.start()
         loads[key] = copy
 
-    stores = []
-
-    def store(src, dst):
-        copy = pltpu.make_async_copy(src, dst, osem.at[len(stores)])
-        copy.start()
-        stores.append(copy)
-
     class Scatter:
         def __init__(self, axis, own, landing, add, need=None):
             self.axis, self.own, self.landing, self.add, self.need = axis, own, landing, add, need
@@ -144,29 +138,20 @@
         else:
             load((f, h, k), (gg, gu)[h].at[1, :, at("y", k)], G.at[h, 1, :, at("y", k)])
 
-    def load_down(h, k):
-        load((2, h, k % 8), gd.at[h, at("z", k)], GD.at[h, at("z", k)])
-
-    for f in BOTH:
-        for h in BOTH:
+    for h in BOTH:
+        for f in BOTH:
             load_wide(f, h, 2)
-    for h in BOTH:
-        load_down(h, 4)
-    for f in BOTH:
-        for h, k in ((1, 1), (0, 3)):
+    for i in BOTH:
+        load(("down", i), gd.at[i], GR.at[i])
+    for h, k in ((1, 1), (0, 3), (0, 1), (1, 3), (0, 0), (1, 0)):
+        for f in BOTH:
             load_wide(f, h, k)
-    for h, k in ((1, 3), (0, 5), (0, 3), (1, 5), (1, 2), (0, 6), (0, 2), (1, 6)):
-        load_down(h, k)
-    for f in BOTH:
-        for h, k in ((0, 1), (1, 3)):
-            load_wide(f, h, k)
-    for h, k in ((0, 1), (1, 7), (1, 1), (0, 7)):
-        load_down(h, k)
-    for f in BOTH:
-        for h in BOTH:
-            load_wide(f, h, 0)
-    for h in BOTH:
-        load_down(h, 0)
+    mine = pl.multiple_of(8 * (d // 2), 8)
+    low = pl.multiple_of(8 * ((11 * d) // 8) - 8 * (d // 127), 8)
+    own_w = [pltpu.make_async_copy(w.at[:, pl.ds(mine, 8), :], OW.at[i], wsem.at[i]) for i, w in enumerate((wg, wu))]
+    own_w.append(pltpu.make_async_copy(wd.at[:, pl.ds(low, 24), :], OWD, wsem.at[2]))
+    for copy in own_w:
+        copy.start()
     ready = set()
 
     def need(f, n):
@@ -182,6 +167,26 @@
     barrier = pltpu.get_barrier_semaphore()
     for a, k in partners:
         pl.semaphore_signal(barrier, inc=1, device_id=device(a, k), device_id_type=pl.DeviceIdType.MESH)
+
+    row = lax.broadcasted_iota(jnp.int32, (ROWS, 128), 0)
+    lane = lax.broadcasted_iota(jnp.int32, (ROWS, 128), 1)
+
+    def split(i, n):
+        q = (i * (2**18 // n + 1)) >> 18
+        return q, i - q * n
+
+    zz, rest = split(row, 88)
+    yy, rest = split(rest, 22)
+    layer, r = split(rest, 11)
+    forth = layer * 352 + yy * 88 + zz * 11 + r
+    layer, rest = split(row, 352)
+    yy, rest = split(rest, 88)
+    zz, r = split(rest, 11)
+    back = zz * 88 + yy * 22 + layer * 11 + r
+    for ref, there in ((PF, forth), (PB, back)):
+        for c in range(0, ROWS, 128):
+            n = min(128, ROWS - c)
+            ref[:, c : c + n] = jnp.where(there == lane + c, 1.0, 0.0).astype(bf16)[:, :n]
     pl.semaphore_wait(barrier, len(partners))
 
     def wide(f):
@@ -211,7 +216,7 @@
         loop(4, body)
 
     first = [Scatter("xy"[f], wide(f), L1.at[f], add_wide(f), need(f, 4)) for f in BOTH]
-    down = Scatter("z", lambda h, k: GD.at[h, at("z", k)], LZ, add_down, need(2, 8))
+    down = Scatter("z", lambda h, k: GD.at[h, at("z", k)], LZ, add_down)
 
     def end_wide(f, h):
         a, b = first[f].last(h)
@@ -228,7 +233,6 @@
 
     def end_down(h):
         a, b = down.last(h)
-        need(2, 8)(h, 0)
         own = GD.at[h, at("z", 0)]
 
         def body(i):
@@ -279,13 +283,21 @@
     for f in BOTH:
         for h, s in LONG:
             first[f].first(h, s)
-    for h, s in LONG:
-        down.first(h, s)
     for f in BOTH:
         for h, s in SHORT:
             first[f].first(h, s)
-    for h, s in SHORT:
-        down.first(h, s)
+    for i in BOTH:
+        loads["down", i].wait()
+
+    def permute(i):
+        rows = GR[:, pl.ds(pl.multiple_of(i * 352, 32), 352), :].reshape(ROWS, 512)
+        out = jnp.dot(PF[...], rows, preferred_element_type=f32)
+        for zz in range(Z):
+            for h in BOTH:
+                GD[h, zz, i] = out[88 * zz : 88 * zz + 88, 256 * h : 256 * h + 256].astype(bf16)
+
+    loop(4, permute)
+    down.start()
     arrive_pair(down, 1)
     arrive_pair(down, 1, True)
     arrive_pair(first[0], 1)
@@ -362,21 +374,27 @@
     def adamw(w, m, v, g):
         m = 0.9 * m + 0.1 * g
         v = 0.95 * v + 0.05 * g * g
-        return (w - 0.02 * (m * lax.rsqrt(v + 1e-8) + 0.1 * w)).astype(bf16), m, v
-
-    for h, (w_, m_, v_, om, ov) in enumerate(((wg, mg, vg, omg, ovg), (wu, mu, vu, omu, ovu))):
-        w, m, v = (jnp.concatenate([r[0].astype(f32), r[1].astype(f32)], 0) for r in (w_, m_, v_))
-        w, m, v = adamw(w, m, v, g_wide[h] * factor)
-        WZ[z, h] = w
-        for layer in BOTH:
-            om[layer] = m[4 * layer : 4 * layer + 4]
-            ov[layer] = v[4 * layer : 4 * layer + 4]
+        return (w - 0.02 * (m * lax.rsqrt(v + 1e-8) + 0.1 * w)).astype(bf16)
+
+    for copy in own_w:
+        copy.wait()
+    odd = d % 2 == 1
+    for h, (m_, v_) in enumerate(((mg, vg), (mu, vu))):
+        w = [OW[h, i].astype(f32) for i in BOTH]
+        w = jnp.concatenate([jnp.where(odd, one[4:], one[:4]) for one in w], 0)
+        m, v = (jnp.concatenate([r[0], r[1]], 0) for r in (m_, v_))
+        g = g_wide[h] * factor
+        gwide[h] = g
+        WZ[z, h] = adamw(w, m, v, g)
     g = jnp.concatenate(g_down, 1) * factor
+    gdown[...] = g
     for h in BOTH:
         DS[h, :24] = jnp.zeros((24, 256), f32)
+    pick = lax.broadcasted_iota(jnp.int32, (24, 24), 1) == lax.broadcasted_iota(jnp.int32, (24, 24), 0) + (11 * d - low)
+    pick = jnp.where(pick, 1.0, 0.0).astype(bf16)
     for layer in BOTH:
-        w, m, v = adamw(wd[layer].astype(f32), md[layer], vd[layer], g[11 * layer : 11 * layer + 11])
-        omd[layer], ovd[layer] = m, v
+        w = jnp.dot(pick, OWD[layer], preferred_element_type=f32)[:11]
+        w = adamw(w, md[:, layer, :], vd[:, layer, :], g[11 * layer : 11 * layer + 11])
         for h in BOTH:
             DS[h, 11 * layer : 11 * layer + 11, :] = w[:, 256 * h : 256 * h + 256].astype(f32)
     for h in BOTH:
@@ -409,16 +427,6 @@
     down_z = Gather("z", lambda h, k: WD.at[h, at("z", k)])
     down_z.start()
 
-    def put_wide(f, h, k):
-        out = (og, ou)[h]
-        if f == 0:
-            store(WG.at[h, 0, at("x", k)], out.at[0, at("x", k)])
-        else:
-            store(WG.at[h, 1, :, at("y", k)], out.at[1, :, at("y", k)])
-
-    def put_down(h, k):
-        store(WD.at[h, at("z", k)], od.at[h, at("z", k)])
-
     for ring in near:
         arrive_pair(ring, 1)
     for ring in near:
@@ -427,53 +435,65 @@
     for f in BOTH:
         arrive_pair(near[f], 2)
         far_rings[f].start()
-    for h in BOTH:
-        put_down(h, 0)
-        for f in BOTH:
-            put_wide(f, h, 0)
-
-    def down_arrive(t, short=False):
-        for h, s in SHORT if short else LONG:
-            put_down(h, down_z.arrive(h, s, t))
-
-    def wide_arrive(t, short=False):
-        for f in BOTH:
-            for h, s in SHORT if short else LONG:
-                put_wide(f, h, far_rings[f].arrive(h, s, t))
-
-    down_arrive(1)
-    down_arrive(1, True)
-    down_arrive(2)
-    wide_arrive(1)
-    down_arrive(2, True)
-    down_arrive(3)
-    wide_arrive(1, True)
-    down_arrive(3, True)
-    down_arrive(4)
-    wide_arrive(2)
+    arrive_pair(down_z, 1)
+    arrive_pair(down_z, 1, True)
+    arrive_pair(down_z, 2)
+    for f in BOTH:
+        arrive_pair(far_rings[f], 1)
+    arrive_pair(down_z, 2, True)
+    arrive_pair(down_z, 3)
+    for f in BOTH:
+        arrive_pair(far_rings[f], 1, True)
+    arrive_pair(down_z, 3, True)
+    arrive_pair(down_z, 4)
+
+    def restore(i):
+        for h in BOTH:
+            rows = WD[h, :, i].astype(f32).reshape(ROWS, 256).astype(bf16)
+            out = jnp.dot(PB[...], rows, preferred_element_type=f32).astype(bf16)
+            for layer in BOTH:
+                OD[layer, pl.ds(pl.multiple_of(i * 352, 32), 352), 256 * h : 256 * h + 256] = out[352 * layer : 352 * layer + 352]
+
+    loop(4, restore)
+    for f in BOTH:
+        arrive_pair(far_rings[f], 2)
     for copy in pending:
         copy.wait_send()
-    for copy in stores:
+
+
+def finish(W, OD, gwide, gdown, mg, mu, md, vg, vu, vd, og, ou, od, omg, omu, omd, ovg, ovu, ovd, sem):
+    copies = [pltpu.make_async_copy(src, dst, sem.at[i]) for i, (src, dst) in enumerate(((W.at[0], og), (W.at[1], ou), (OD, od)))]
+    for copy in copies:
+        copy.start()
+
+    def moments(m, v, g):
+        return 0.9 * m + 0.1 * g, 0.95 * v + 0.05 * g * g
+
+    for layer in BOTH:
+        for h, (m, v, om, ov) in enumerate(((mg, vg, omg, ovg), (mu, vu, omu, ovu))):
+            om[layer], ov[layer] = moments(m[layer], v[layer], gwide[h, 4 * layer : 4 * layer + 4, :])
+        m, v = moments(md[:, layer, :], vd[:, layer, :], gdown[11 * layer : 11 * layer + 11, :])
+        omd[:, layer, :] = m
+        ovd[:, layer, :] = v
+    for copy in copies:
         copy.wait()
 
 
 def step_kernel(*args):
     hbm, vmem = pl.BlockSpec(memory_space=pl.ANY), pl.BlockSpec(memory_space=pltpu.VMEM)
-    wide, deep = (2, 4, F), (2, 11, 512)
+    wide, deep = (2, 4, F), (11, 2, 512)
     unit, half = (4, 32, F), (4, 88, 256)
     pair, square, whole_down = (2, 2), (4, *unit), (2, 8, *half)
     blocks, small, tile = (8, 2, 8, F), (4, 2, 24, 256), (8, 128)
     shape = jax.ShapeDtypeStruct
-    return pl.pallas_call(
+    out = pl.pallas_call(
         kernel,
-        out_shape=(
-            shape((2, *square), bf16), shape((2, *square), bf16), shape(whole_down, bf16),
-            shape(wide, f32), shape(wide, f32), shape(deep, f32), shape(wide, f32), shape(wide, f32), shape(deep, f32),
-        ),
-        in_specs=[hbm] * 3 + [vmem] * 9,
-        out_specs=(hbm,) * 3 + (vmem,) * 6,
+        out_shape=(pltpu.VMEM((*pair, *square), bf16), pltpu.VMEM((2, F, 512), bf16), pltpu.VMEM(blocks[1:], f32), pltpu.VMEM((24, 512), f32)),
+        in_specs=[hbm] * 6 + [vmem] * 6,
+        out_specs=(vmem,) * 4,
         scratch_shapes=[
             pltpu.VMEM((*pair, *square), bf16),
+            pltpu.VMEM((2, F, 512), bf16),
             pltpu.VMEM(whole_down, bf16),
             pltpu.VMEM((2, 6, *unit), bf16),
             pltpu.VMEM((*pair, *unit), f32),
@@ -493,30 +513,41 @@
             pltpu.VMEM(small, bf16),
             pltpu.VMEM((3, *tile), f32),
             pltpu.VMEM((3, 8, *tile), f32),
-            pltpu.VMEM((*pair, *square), bf16),
             pltpu.VMEM(whole_down, bf16),
             pltpu.VMEM(blocks, bf16),
             pltpu.VMEM(small, bf16),
+            pltpu.VMEM((ROWS, ROWS), bf16),
+            pltpu.VMEM((ROWS, ROWS), bf16),
+            pltpu.VMEM((*pair, 8, F), bf16),
+            pltpu.VMEM((2, 24, 512), bf16),
             pltpu.SemaphoreType.DMA((SEMS,)),
             pltpu.SemaphoreType.DMA((SEMS,)),
             pltpu.SemaphoreType.DMA((LOADS,)),
-            pltpu.SemaphoreType.DMA((LOADS,)),
+            pltpu.SemaphoreType.DMA((3,)),
         ],
-        compiler_params=pltpu.CompilerParams(collective_id=0, has_side_effects=True, vmem_limit_bytes=60 * 2**20),
+        compiler_params=pltpu.CompilerParams(collective_id=0, has_side_effects=True, vmem_limit_bytes=40 * 2**20),
         name="clipped_step",
     )(*args)
+    out = [pltpu.with_memory_space_constraint(one, pltpu.VMEM) for one in out]
+    return pl.pallas_call(
+        finish,
+        out_shape=(shape((2, *square), bf16),) * 2 + (shape((2, F, 512), bf16),) + (shape(wide, f32), shape(wide, f32), shape(deep, f32)) * 2,
+        in_specs=[vmem] * 10,
+        out_specs=(hbm,) * 3 + (vmem,) * 6,
+        scratch_shapes=[pltpu.SemaphoreType.DMA((3,))],
+        compiler_params=pltpu.CompilerParams(vmem_limit_bytes=40 * 2**20),
+        name="finish",
+    )(*out, *args[6:])
 
 
 def solution(mesh):
-    def step(gg, gu, gd, wg, wu, wd, *moments):
+    def step(gg, gu, gd, wg, wu, wd, mg, mu, md, vg, vu, vd):
         gg, gu = (g.reshape(2, 4, 4, 32, F) for g in (gg, gu))
-        gd = gd.reshape(2, 4, 4, 8, 11, 2, 256).transpose(5, 3, 1, 2, 0, 4, 6).reshape(2, 8, 4, 88, 256)
-        me = lax.axis_index("dp")
-        own = [lax.dynamic_slice_in_dim(w, me * n, n, 1) for w, n in ((wg, 4), (wu, 4), (wd, 11))]
-        og, ou, od, *rest = step_kernel(gg, gu, gd, *own, *moments)
+        md, vd = (a.transpose(1, 0, 2) for a in (md, vd))
+        og, ou, od, omg, omu, omd, ovg, ovu, ovd = step_kernel(gg, gu, gd[0], wg, wu, wd, mg, mu, md, vg, vu, vd)
         og, ou = (o.reshape(2, 512, F) for o in (og, ou))
-        od = od.reshape(2, 8, 4, 4, 2, 11, 256).transpose(4, 2, 3, 1, 5, 0, 6).reshape(2, F, 512)
-        return (og, ou, od, *rest)
+        omd, ovd = (a.transpose(1, 0, 2) for a in (omd, ovd))
+        return og, ou, od, omg, omu, omd, ovg, ovu, ovd
 
     all_of, cut = P(None, None, None), P(None, "dp", None)
     return jax.shard_map(

time: 159 us -> 128 us (0.81)
  local copies, waits for them, and re-layouts: 44.4 us -> 6.54 us
  Pallas kernels: 113 us -> 119 us
    reshape x3 -> x0, local copies, waits for them, and re-layouts: 16.6 us -> none  [the longest x2 9.16 us: step(): gd.reshape(2, 4, 4, 8, 11, 2, 256).transpose(5, 3, 1, 2, 0, 4, 6)]
    unnamed x22 -> x14, local copies, waits for them, and re-layouts: 15.5 us -> 6.54 us
    transpose x2 -> x0, local copies, waits for them, and re-layouts: 6.79 us -> none  [the longest x1 4.54 us: step(): od.reshape(2, 8, 4, 4, 2, 11, 256).transpose(4, 2, 3, 1, 5, 0, 6)]
    pallas_call x1 -> x2, Pallas kernels: 113 us -> 119 us  [the longest x1 115 us: step_kernel(): pl.pallas_call(kernel, out_shape=(pltpu.VMEM((*pair, *square), bf16), plt...]
    pallas_call x1 -> x0, local copies, waits for them, and re-layouts: 3.44 us -> none  [step_kernel(): pl.pallas_call(kernel, out_shape=(shape((2, *square), bf16), shape((2, *s...]
    dynamic_slice x2 -> x0, local copies, waits for them, and re-layouts: 2.08 us -> none  [step(): lax.dynamic_slice_in_dim(w, me * n, n, 1)]
where the time goes in v2:
time: 128 us; the launch traced here: 127 us
  Pallas kernels  119 us (93%)
  local copies, waits for them, and re-layouts  6.54 us (5%)
    pallas_call x1, Pallas kernels, step_kernel(): pl.pallas_call(kernel, out_shape=(pltpu.VMEM((*pair, *square), bf16), plt...  115 us
    unnamed x14, local copies, waits for them, and re-layouts  6.54 us
    pallas_call x1, Pallas kernels, step_kernel(): pl.pallas_call(finish, out_shape=(shape((2, *square), bf16),) * 2 + (shap...  4.21 us

profile of v2, /device:TPU:2, one launch (start us, length us, event | category | flops | bytes accessed | tf_op | source)
XLA Modules:
  0.0 126.5 jit_solution(10727035310376456501)
XLA Ops:
  0.6 0.0 copy-start
  0.7 1.8 %copy-done = bf16[1,2,512,1408]{3,2,1,0:T(8,128)(2,1)S(1)} copy-done((bf16[1,2,512,1408]{3,2,1,0:T(8,128)(2,1)S(1)}, bf16[1,2,512,1408]{3,2,1,0:T(8,128)(2,1)}, u32[]{:S(2)}) %copy-start) | copy-done | bytes 2883608
  2.5 0.0 copy-start.1
  2.5 0.8 copy-done.1
  3.3 0.0 copy-start.2
  3.3 0.8 copy-done.2
  4.0 0.0 copy-start.3
  4.0 0.8 copy-done.3
  4.8 0.0 copy-start.4
  4.8 0.8 copy-done.4
  5.6 0.0 copy-start.5
  5.6 0.8 copy-done.5
  6.4 0.0 copy-start.6
  6.4 0.8 copy-done.6
  7.2 115.1 %clipped_step.1 = (bf16[2,2,4,4,32,1408]{5,4,3,2,1,0:T(8,128)(2,1)S(1)}, bf16[2,1408,512]{2,1,0:T(8,128)(2,1)S(1)}, f32[2,8,1408]{2,1,0:T(8,128)S(1)}, f32[24,512]{1,0:T(8,128)S(1)}) custom-call(bf16[2,4,4,32,1408]{4,3,2,1,0:T(8,128)(2,1)S(1)} %bitcast.9, bf16[2,4,4,32,1408]{4,3,2,1,0:T(8,128)(2,1)} %bitcast.14, bf16[2,1408,512]{2,1,0:T(8,128)(2,1)} %bitcast.15, ...), custom_call_target="tpu_custom_call" | custom-call | tf_op jit(solution)/shard_map/clipped_step/pallas_call | solution.py:489
  122.3 4.2 %finish.1 = (bf16[2,4,4,32,1408]{4,3,2,1,0:T(8,128)(2,1)}, bf16[2,4,4,32,1408]{4,3,2,1,0:T(8,128)(2,1)}, bf16[2,1408,512]{2,1,0:T(8,128)(2,1)}, f32[2,4,1408]{2,...) custom-call(bf16[2,2,4,4,32,1408]{5,4,3,2,1,0:T(8,128)(2,1)S(1)} %ge, ...), custom_call_target="tpu_custom_call" | custom-call | tf_op jit(solution)/shard_map/finish/pallas_call | solution.py:532
Async XLA Ops:
  0.6 1.8 %copy-start = (bf16[1,2,512,1408]{3,2,1,0:T(8,128)(2,1)S(1)}, bf16[1,2,512,1408]{3,2,1,0:T(8,128)(2,1)}, u32[]{:S(2)}) copy-start(bf16[1,2,512,1408]{3,2,1,0:T(8,128)(2,1)} %param.12) | copy-start | bytes 8650756
  2.5 0.8 copy-start.1
  3.3 0.8 copy-start.2
  4.0 0.8 copy-start.3
  4.8 0.8 copy-start.4
  5.6 0.8 copy-start.5
  6.4 0.8 copy-start.6

commit v3 on v2

--- a/solution.py
+++ b/solution.py
@@ -40,8 +40,8 @@
     lax.fori_loop(0, n, step, 0)
 
 
-def kernel(gg, gu, gd, wg, wu, wd, mg, mu, md, vg, vu, vd, WG, OD, gwide, gdown, *scratch):
-    (G, GR, GD, L1, F1, B1, L2, F2, ZS, ZF, ZL, LZ, FD, BD, LDX, DS, YS, YF, YL, NS, NL, WD, WZ, YW, PF, PB, OW, OWD) = scratch[:-4]
+def kernel(gg, gu, gd, wg, wu, wd, mg, mu, md, vg, vu, vd, WG, OD, MW, MD, *scratch):
+    (G, GR, GD, L1, F1, B1, L2, F2, ZS, ZF, ZL, LZ, FD, BD, LDX, DS, YS, YF, YL, NS, NL, WD, WZ, YW, PF, PB, OW, OWD, IW, ID) = scratch[:-4]
     ssem, rsem, lsem, wsem = scratch[-4:]
     d = lax.axis_index("dp")
     x, y, z = d // 32, (d // 8) % 4, d % 8
@@ -150,6 +150,10 @@
     low = pl.multiple_of(8 * ((11 * d) // 8) - 8 * (d // 127), 8)
     own_w = [pltpu.make_async_copy(w.at[:, pl.ds(mine, 8), :], OW.at[i], wsem.at[i]) for i, w in enumerate((wg, wu))]
     own_w.append(pltpu.make_async_copy(wd.at[:, pl.ds(low, 24), :], OWD, wsem.at[2]))
+    for i, (wide_, deep_) in enumerate((((mg, mu), md), ((vg, vu), vd))):
+        for h in BOTH:
+            own_w.append(pltpu.make_async_copy(wide_[h], IW.at[i, h], wsem.at[len(own_w)]))
+        own_w.append(pltpu.make_async_copy(deep_, ID.at[i], wsem.at[len(own_w)]))
     for copy in own_w:
         copy.start()
     ready = set()
@@ -374,27 +378,29 @@
     def adamw(w, m, v, g):
         m = 0.9 * m + 0.1 * g
         v = 0.95 * v + 0.05 * g * g
-        return (w - 0.02 * (m * lax.rsqrt(v + 1e-8) + 0.1 * w)).astype(bf16)
+        return (w - 0.02 * (m * lax.rsqrt(v + 1e-8) + 0.1 * w)).astype(bf16), m, v
 
     for copy in own_w:
         copy.wait()
     odd = d % 2 == 1
-    for h, (m_, v_) in enumerate(((mg, vg), (mu, vu))):
+    for h in BOTH:
         w = [OW[h, i].astype(f32) for i in BOTH]
         w = jnp.concatenate([jnp.where(odd, one[4:], one[:4]) for one in w], 0)
-        m, v = (jnp.concatenate([r[0], r[1]], 0) for r in (m_, v_))
-        g = g_wide[h] * factor
-        gwide[h] = g
-        WZ[z, h] = adamw(w, m, v, g)
+        m, v = (jnp.concatenate([IW[i, h, 0], IW[i, h, 1]], 0) for i in BOTH)
+        WZ[z, h], *new = adamw(w, m, v, g_wide[h] * factor)
+        for i, one in enumerate(new):
+            for layer in BOTH:
+                MW[i, h, layer] = one[4 * layer : 4 * layer + 4]
     g = jnp.concatenate(g_down, 1) * factor
-    gdown[...] = g
     for h in BOTH:
         DS[h, :24] = jnp.zeros((24, 256), f32)
     pick = lax.broadcasted_iota(jnp.int32, (24, 24), 1) == lax.broadcasted_iota(jnp.int32, (24, 24), 0) + (11 * d - low)
     pick = jnp.where(pick, 1.0, 0.0).astype(bf16)
     for layer in BOTH:
         w = jnp.dot(pick, OWD[layer], preferred_element_type=f32)[:11]
-        w = adamw(w, md[:, layer, :], vd[:, layer, :], g[11 * layer : 11 * layer + 11])
+        w, *new = adamw(w, ID[0, :, layer, :], ID[1, :, layer, :], g[11 * layer : 11 * layer + 11])
+        for i, one in enumerate(new):
+            MD[i, :, layer, :] = one
         for h in BOTH:
             DS[h, 11 * layer : 11 * layer + 11, :] = w[:, 256 * h : 256 * h + 256].astype(f32)
     for h in BOTH:
@@ -461,20 +467,12 @@
         copy.wait_send()
 
 
-def finish(W, OD, gwide, gdown, mg, mu, md, vg, vu, vd, og, ou, od, omg, omu, omd, ovg, ovu, ovd, sem):
-    copies = [pltpu.make_async_copy(src, dst, sem.at[i]) for i, (src, dst) in enumerate(((W.at[0], og), (W.at[1], ou), (OD, od)))]
+def finish(W, OD, MW, MD, *rest):
+    sem = rest[-1]
+    sources = [W.at[0], W.at[1], OD] + [r for i in BOTH for r in (MW.at[i, 0], MW.at[i, 1], MD.at[i])]
+    copies = [pltpu.make_async_copy(src, dst, sem.at[i]) for i, (src, dst) in enumerate(zip(sources, rest))]
     for copy in copies:
         copy.start()
-
-    def moments(m, v, g):
-        return 0.9 * m + 0.1 * g, 0.95 * v + 0.05 * g * g
-
-    for layer in BOTH:
-        for h, (m, v, om, ov) in enumerate(((mg, vg, omg, ovg), (mu, vu, omu, ovu))):
-            om[layer], ov[layer] = moments(m[layer], v[layer], gwide[h, 4 * layer : 4 * layer + 4, :])
-        m, v = moments(md[:, layer, :], vd[:, layer, :], gdown[11 * layer : 11 * layer + 11, :])
-        omd[:, layer, :] = m
-        ovd[:, layer, :] = v
     for copy in copies:
         copy.wait()
 
@@ -488,8 +486,8 @@
     shape = jax.ShapeDtypeStruct
     out = pl.pallas_call(
         kernel,
-        out_shape=(pltpu.VMEM((*pair, *square), bf16), pltpu.VMEM((2, F, 512), bf16), pltpu.VMEM(blocks[1:], f32), pltpu.VMEM((24, 512), f32)),
-        in_specs=[hbm] * 6 + [vmem] * 6,
+        out_shape=(pltpu.VMEM((*pair, *square), bf16), pltpu.VMEM((2, F, 512), bf16), pltpu.VMEM((*pair, *wide), f32), pltpu.VMEM((2, *deep), f32)),
+        in_specs=[hbm] * 12,
         out_specs=(vmem,) * 4,
         scratch_shapes=[
             pltpu.VMEM((*pair, *square), bf16),
@@ -520,24 +518,26 @@
             pltpu.VMEM((ROWS, ROWS), bf16),
             pltpu.VMEM((*pair, 8, F), bf16),
             pltpu.VMEM((2, 24, 512), bf16),
+            pltpu.VMEM((*pair, *wide), f32),
+            pltpu.VMEM((2, *deep), f32),
             pltpu.SemaphoreType.DMA((SEMS,)),
             pltpu.SemaphoreType.DMA((SEMS,)),
             pltpu.SemaphoreType.DMA((LOADS,)),
-            pltpu.SemaphoreType.DMA((3,)),
+            pltpu.SemaphoreType.DMA((9,)),
         ],
-        compiler_params=pltpu.CompilerParams(collective_id=0, has_side_effects=True, vmem_limit_bytes=40 * 2**20),
+        compiler_params=pltpu.CompilerParams(collective_id=0, has_side_effects=True, vmem_limit_bytes=50 * 2**20),
         name="clipped_step",
     )(*args)
     out = [pltpu.with_memory_space_constraint(one, pltpu.VMEM) for one in out]
     return pl.pallas_call(
         finish,
         out_shape=(shape((2, *square), bf16),) * 2 + (shape((2, F, 512), bf16),) + (shape(wide, f32), shape(wide, f32), shape(deep, f32)) * 2,
-        in_specs=[vmem] * 10,
-        out_specs=(hbm,) * 3 + (vmem,) * 6,
-        scratch_shapes=[pltpu.SemaphoreType.DMA((3,))],
-        compiler_params=pltpu.CompilerParams(vmem_limit_bytes=40 * 2**20),
+        in_specs=[vmem] * 4,
+        out_specs=(hbm,) * 9,
+        scratch_shapes=[pltpu.SemaphoreType.DMA((9,))],
+        compiler_params=pltpu.CompilerParams(vmem_limit_bytes=50 * 2**20),
         name="finish",
-    )(*out, *args[6:])
+    )(*out)
 
 
 def solution(mesh):

time: 128 us -> 119 us (0.930); the launches traced: 127 us -> 119 us
  local copies, waits for them, and re-layouts: 6.54 us -> 0 us
    unnamed x14 -> x0, local copies, waits for them, and re-layouts: 6.54 us -> none
where the time goes in v3:
time: 119 us
  Pallas kernels  118 us (99%)
    pallas_call x1, Pallas kernels, step_kernel(): pl.pallas_call(kernel, out_shape=(pltpu.VMEM((*pair, *square), bf16), plt...  115 us
    pallas_call x1, Pallas kernels, step_kernel(): pl.pallas_call(finish, out_shape=(shape((2, *square), bf16),) * 2 + (shap...  3.57 us

profile of v3, /device:TPU:2, one launch (start us, length us, event | category | flops | bytes accessed | tf_op | source)
XLA Modules:
  0.0 118.9 jit_solution(15116318417725366387)
XLA Ops:
  0.6 114.7 %clipped_step.1 = (bf16[2,2,4,4,32,1408]{5,4,3,2,1,0:T(8,128)(2,1)S(1)}, bf16[2,1408,512]{2,1,0:T(8,128)(2,1)S(1)}, f32[2,2,2,4,1408]{4,3,2,1,0:T(4,128)S(1)}, f32[2,11,2,512]{3,2,1,0:T(2,128)S(1)}) custom-call(bf16[2,4,4,32,1408]{4,3,2,1,0:T(8,128)(2,1)} %bitcast.9, bf16[2,4,4,32,1408]{4,3,2,1,0:T(8,128)(2,1)} %bitcast.10, bf16[2,1408,512]{2,1,0:T(8,128)(2,1)} %bitcast.11, ...), custom_call_target="tpu_custom_call" | custom-call | tf_op jit(solution)/shard_map/clipped_step/pallas_call | solution.py:487
  115.3 3.6 %finish.1 = (bf16[2,4,4,32,1408]{4,3,2,1,0:T(8,128)(2,1)}, bf16[2,4,4,32,1408]{4,3,2,1,0:T(8,128)(2,1)}, bf16[2,1408,512]{2,1,0:T(8,128)(2,1)}, f32[2,4,1408]{2,...) custom-call(bf16[2,2,4,4,32,1408]{5,4,3,2,1,0:T(8,128)(2,1)S(1)} %ge, ...), custom_call_target="tpu_custom_call" | custom-call | tf_op jit(solution)/shard_map/finish/pallas_call | solution.py:532

commit v4 on v3

--- a/solution.py
+++ b/solution.py
@@ -28,10 +28,6 @@
     return {key: i for i, key in enumerate((h, s, t) for h, s, length in chains(n) for t in range(1, length + 1))}
 
 
-def sixteen(i):
-    return pl.ds(pl.multiple_of(i * 16, 16), 16)
-
-
 def loop(n, body):
     def step(i, carry):
         body(i)
@@ -41,8 +37,8 @@
 
 
 def kernel(gg, gu, gd, wg, wu, wd, mg, mu, md, vg, vu, vd, WG, OD, MW, MD, *scratch):
-    (G, GR, GD, L1, F1, B1, L2, F2, ZS, ZF, ZL, LZ, FD, BD, LDX, DS, YS, YF, YL, NS, NL, WD, WZ, YW, PF, PB, OW, OWD, IW, ID) = scratch[:-4]
-    ssem, rsem, lsem, wsem = scratch[-4:]
+    (G, GR, GD, L1, F1, B1, L2, F2, ZS, ZF, ZL, LZ, DS, YS, YF, YL, NS, NL, WD, WZ, YW, PF, PB, OW, OWD, IW, ID) = scratch[:-5]
+    ssem, rsem, lsem, wsem, nsem = scratch[-5:]
     d = lax.axis_index("dp")
     x, y, z = d // 32, (d // 8) % 4, d % 8
     place = {"x": (x, 4), "y": (y, 4), "z": (z, 8)}
@@ -53,21 +49,29 @@
 
     def device(axis, k):
         p = at(axis, k)
-        return {"dp": {"x": p * 32 + y * 8 + z, "y": x * 32 + p * 8 + z, "z": x * 32 + y * 8 + p}[axis]}
+        return {"x": p * 32 + y * 8 + z, "y": x * 32 + p * 8 + z, "z": x * 32 + y * 8 + p}[axis]
 
     used = [0]
     pending = []
 
-    def send(src, dst, axis, k):
+    def send_to(target, src, dst):
         i = used[0]
         used[0] += 1
         copy = pltpu.make_async_remote_copy(
             src_ref=src, dst_ref=dst, send_sem=ssem.at[i], recv_sem=rsem.at[i],
-            device_id=device(axis, k), device_id_type=pl.DeviceIdType.MESH,
+            device_id={"dp": target}, device_id_type=pl.DeviceIdType.MESH,
         )
         copy.start()
         pending.append(copy)
         return copy
+
+    def send(src, dst, axis, k):
+        return send_to(device(axis, k), src, dst)
+
+    plane = sorted(((i, j) for i in range(X) for j in range(Y) if i or j), key=lambda o: -sum(min(k, X - k) for k in o))
+
+    def send_plane(source, target):
+        return [send_to(at("x", i) * 32 + at("y", j) * 8 + z, source(i, j), target(i, j)) for i, j in plane]
 
     loads = {}
 
@@ -167,10 +171,10 @@
 
         return wait
 
-    partners = [(a, k) for a, n in (("x", 4), ("y", 4), ("z", 8)) for k in range(1, n)]
     barrier = pltpu.get_barrier_semaphore()
-    for a, k in partners:
-        pl.semaphore_signal(barrier, inc=1, device_id=device(a, k), device_id_type=pl.DeviceIdType.MESH)
+    for axis in place:
+        for way in WAYS:
+            pl.semaphore_signal(barrier, inc=1, device_id={"dp": device(axis, way)}, device_id_type=pl.DeviceIdType.MESH)
 
     row = lax.broadcasted_iota(jnp.int32, (ROWS, 128), 0)
     lane = lax.broadcasted_iota(jnp.int32, (ROWS, 128), 1)
@@ -179,37 +183,52 @@
         q = (i * (2**18 // n + 1)) >> 18
         return q, i - q * n
 
+    def one_hot(ref, there):
+        for c in range(0, ROWS, 128):
+            n = min(128, ROWS - c)
+            ref[:, c : c + n] = jnp.where(there == lane + c, 1.0, 0.0).astype(bf16)[:, :n]
+
     zz, rest = split(row, 88)
     yy, rest = split(rest, 22)
     layer, r = split(rest, 11)
-    forth = layer * 352 + yy * 88 + zz * 11 + r
-    layer, rest = split(row, 352)
-    yy, rest = split(rest, 88)
-    zz, r = split(rest, 11)
-    back = zz * 88 + yy * 22 + layer * 11 + r
-    for ref, there in ((PF, forth), (PB, back)):
-        for c in range(0, ROWS, 128):
-            n = min(128, ROWS - c)
-            ref[:, c : c + n] = jnp.where(there == lane + c, 1.0, 0.0).astype(bf16)[:, :n]
-    pl.semaphore_wait(barrier, len(partners))
-
-    def wide(f):
-        def own(h, k):
-            return G.at[h, 0, at("x", k)] if f == 0 else G.at[h, 1, :, at("y", k)]
-
-        return own
-
-    def add_wide(f):
+    one_hot(PF, layer * 352 + yy * 88 + zz * 11 + r)
+    pl.semaphore_wait(barrier, 2 * len(place))
+
+    def unit(ref, f, h, k, j):
+        return ref.at[h, 0, at("x", k), at("y", j)] if f == 0 else ref.at[h, 1, at("x", j), at("y", k)]
+
+    def by_rows(body):
+        loop(2, lambda i: body(pl.ds(pl.multiple_of(i * 16, 16), 16)))
+
+    def first_stage(f, j):
         def add(got, h, k):
-            own = wide(f)(h, k)
-
-            def body(i):
-                rows = (i // 2, sixteen(i % 2))
+            own = unit(G, f, h, k, j)
+
+            def body(rows):
                 got[rows] = (got[rows].astype(f32) + own[rows].astype(f32)).astype(bf16)
 
-            loop(8, body)
-
-        return add
+            by_rows(body)
+
+        return Scatter("xy"[f], lambda h, k: unit(G, f, h, k, j), L1.at[f, j], add, need(f, 4))
+
+    first = [[first_stage(f, j) for j in range(4)] for f in BOTH]
+
+    def end_first(f, j):
+        for h in BOTH:
+            a, b = first[f][j].last(h)
+            need(f, 4)(h, 0)
+            own = unit(G, f, h, 0, j)
+            place_j = at("yx"[f], j)
+            travels = j == 2 or j == (3, 1)[h]
+
+            def body(rows):
+                total = own[rows].astype(f32) + a[rows].astype(f32) + b[rows].astype(f32)
+                if travels:
+                    B1[f, h, place_j, rows] = total.astype(bf16)
+                else:
+                    F1[f, h, place_j, rows] = total
+
+            by_rows(body)
 
     def add_down(got, h, k):
         own = GD.at[h, at("z", k)]
@@ -219,77 +238,63 @@
 
         loop(4, body)
 
-    first = [Scatter("xy"[f], wide(f), L1.at[f], add_wide(f), need(f, 4)) for f in BOTH]
     down = Scatter("z", lambda h, k: GD.at[h, at("z", k)], LZ, add_down)
-
-    def end_wide(f, h):
-        a, b = first[f].last(h)
-        need(f, 4)(h, 0)
-        own = wide(f)(h, 0)
-
-        def body(i):
-            rows = (i // 2, sixteen(i % 2))
-            total = own[rows].astype(f32) + a[rows].astype(f32) + b[rows].astype(f32)
-            F1[(f, h, *rows)] = total
-            B1[(f, h, *rows)] = total.astype(bf16)
-
-        loop(8, body)
 
     def end_down(h):
         a, b = down.last(h)
         own = GD.at[h, at("z", 0)]
 
         def body(i):
-            total = own[i].astype(f32) + a[i].astype(f32) + b[i].astype(f32)
-            FD[h, i] = total
-            BD[h, i] = total.astype(bf16)
+            DS[h, :88] = own[i].astype(f32) + a[i].astype(f32) + b[i].astype(f32)
+            for j in range(4):
+                block = DS[h, 22 * j : 22 * j + 24, :]
+                YF[i * 4 + j, h] = block
+                YS[i * 4 + j, h] = block.astype(bf16)
 
         loop(4, body)
 
-    def add_second(f):
+    def second_stage(f):
         axis = "yx"[f]
 
         def add(got, h, k):
             own = F1.at[f, h, at(axis, k)]
 
-            def body(i):
-                rows = (sixteen(i),)
+            def body(rows):
                 got[rows] = (got[rows].astype(f32) + own[rows]).astype(bf16)
 
-            loop(2, body)
-
-        return add
-
-    def second_own(f):
-        axis = "yx"[f]
-        return lambda h, k: B1.at[f, h, at(axis, k)]
-
-    def add_down_second(got, h, k):
-        got[...] = (got[...].astype(f32) + FD[h, at("x", k)]).astype(bf16)
-
-    second = [Scatter("yx"[f], second_own(f), L2.at[f], add_second(f)) for f in BOTH]
-    down_second = Scatter("x", lambda h, k: BD.at[h, at("x", k)], LDX, add_down_second)
+            by_rows(body)
+
+        return Scatter(axis, lambda h, k: B1.at[f, h, at(axis, k)], L2.at[f], add)
+
+    second = [second_stage(f) for f in BOTH]
 
     def end_second(f, h):
         a, b = second[f].last(h)
         own = F1.at[f, h, at("yx"[f], 0)]
 
-        def body(i):
-            rows = (sixteen(i),)
-            F2[(f, h, *rows)] = own[rows] + a[rows].astype(f32) + b[rows].astype(f32)
-
-        loop(2, body)
+        def body(rows):
+            F2[f, h, rows] = own[rows] + a[rows].astype(f32) + b[rows].astype(f32)
+
+        by_rows(body)
 
     def arrive_pair(ring, t, short=False):
         for h, s in SHORT if short else LONG:
             ring.arrive(h, s, t)
 
-    for f in BOTH:
-        for h, s in LONG:
-            first[f].first(h, s)
-    for f in BOTH:
-        for h, s in SHORT:
-            first[f].first(h, s)
+    def begin(j, pair):
+        for f in BOTH:
+            for h, s in pair:
+                first[f][j].first(h, s)
+
+    def arrive_first(j):
+        for f in BOTH:
+            arrive_pair(first[f][j], 1)
+
+    order = (2, 1, 3, 0)
+    for j in order:
+        begin(j, LONG)
+    for j in order[:2]:
+        begin(j, SHORT)
     for i in BOTH:
         loads["down", i].wait()
 
@@ -302,23 +307,36 @@
 
     loop(4, permute)
     down.start()
+    for j, later in zip(order, order[2:]):
+        arrive_first(j)
+        begin(later, SHORT)
+    arrive_first(3)
     arrive_pair(down, 1)
+    layer, rest = split(row, 352)
+    yy, rest = split(rest, 88)
+    zz, r = split(rest, 11)
+    one_hot(PB, zz * 88 + yy * 22 + layer * 11 + r)
+    for h in BOTH:
+        DS[h, 88:] = jnp.zeros((8, 256), f32)
     arrive_pair(down, 1, True)
-    arrive_pair(first[0], 1)
-    arrive_pair(first[1], 1)
+    for f in BOTH:
+        end_first(f, 2)
+        for h, s in LONG:
+            second[f].first(h, s)
+    arrive_first(0)
     arrive_pair(down, 2)
+    for f in BOTH:
+        end_first(f, 1)
     arrive_pair(down, 2, True)
+    for f in BOTH:
+        end_first(f, 3)
+        for h, s in SHORT:
+            second[f].first(h, s)
     arrive_pair(down, 3)
     for f in BOTH:
-        for h in BOTH:
-            end_wide(f, h)
-        second[f].start()
-    for h in BOTH:
-        end_down(h)
-    down_second.start()
-    for f in BOTH:
         arrive_pair(second[f], 1)
-    arrive_pair(down_second, 1)
+    for f in BOTH:
+        end_first(f, 0)
     for f in BOTH:
         for h in BOTH:
             end_second(f, h)
@@ -331,25 +349,17 @@
                 ZS[2 * j + i, h] = block.astype(bf16)
     far = (4, 3, 5, 2, 6, 1, 7)
     third = {k: send(ZS.at[at("z", k)], ZL.at[k], "z", k) for k in far}
-
-    for h in BOTH:
-        a, b = down_second.last(h)
-        DS[h, :88] = FD[h, at("x", 0)] + a[...].astype(f32) + b[...].astype(f32)
-        DS[h, 88:] = jnp.zeros((8, 256), f32)
-        for j in range(4):
-            block = DS[h, 22 * j : 22 * j + 24, :]
-            YF[j, h] = block
-            YS[j, h] = block.astype(bf16)
-    third_down = {k: send(YS.at[at("y", k)], YL.at[k], "y", k) for k in (2, 1, 3)}
-
-    for k in (1, 3, 2):
-        third_down[k].wait_recv()
+    for h in BOTH:
+        end_down(h)
+    third_down = send_plane(lambda i, j: YS.at[at("x", i) * 4 + at("y", j)], lambda i, j: YL.at[i * 4 + j])
+    for copy in reversed(third_down):
+        copy.wait_recv()
     real = lax.broadcasted_iota(jnp.int32, (24, 256), 0) < 22
     squares = jnp.zeros((), f32)
     g_down = []
     for h in BOTH:
-        total = YF[y, h]
-        for k in (1, 2, 3):
+        total = YF[x * 4 + y, h]
+        for k in range(1, 16):
             total = total + YL[k, h].astype(f32)
         total = jnp.where(real, total, 0.0).astype(bf16).astype(f32)
         g_down.append(total)
@@ -365,14 +375,24 @@
         g_wide.append(total)
         squares += jnp.sum(total * total)
 
-    total = jnp.full((8, 128), squares, f32)
-    for i, (a, n) in enumerate((("x", 4), ("y", 4), ("z", 8))):
-        NS[i] = total
-        copies = [send(NS.at[i], NL.at[i, k], a, k) for k in range(1, n)]
-        for copy in copies:
-            copy.wait_recv()
-        for k in range(1, n):
-            total = total + NL[i, k]
+    NS[...] = jnp.full((1, 128), squares, f32)
+    NL[0] = NS[...]
+
+    def norm_copy(src, dst, target):
+        return pltpu.make_async_remote_copy(
+            src_ref=src, dst_ref=dst, send_sem=nsem.at[0], recv_sem=nsem.at[1],
+            device_id={"dp": target}, device_id_type=pl.DeviceIdType.MESH,
+        )
+
+    def tell(i):
+        k = lax.rem(i + 63, 127) + 1
+        norm_copy(NS, NL.at[k], lax.rem(d + k, 128)).start()
+
+    loop(127, tell)
+    others = NL.at[pl.ds(1, 127)]
+    told = norm_copy(others, others, device("x", 1))
+    told.wait_recv()
+    total = jnp.sum(NL[...], axis=0)
     factor = jnp.minimum(1.0, 0.5 * lax.rsqrt(total / COUNT + 1e-30))[0:1, 0:1]
 
     def adamw(w, m, v, g):
@@ -404,18 +424,20 @@
         for h in BOTH:
             DS[h, 11 * layer : 11 * layer + 11, :] = w[:, 256 * h : 256 * h + 256].astype(f32)
     for h in BOTH:
-        YW[y, h] = DS[h, :24].astype(bf16)
+        YW[x * 4 + y, h] = DS[h, :24].astype(bf16)
 
     wide_z = {k: send(WZ.at[z], WZ.at[z], "z", k) for k in far}
-    down_y = {k: send(YW.at[y], YW.at[y], "y", k) for k in (2, 1, 3)}
-    for k in (1, 3, 2):
-        down_y[k].wait_recv()
-    for h in BOTH:
-        for j in range(4):
-            DS[h, 22 * j : 22 * j + 24, :] = YW[j, h].astype(f32)
-        WD[h, z, x] = DS[h, :88].astype(bf16)
-    down_x = Gather("x", lambda h, k: WD.at[h, z, at("x", k)])
-    down_x.start()
+    mine = YW.at[x * 4 + y]
+    down_plane = send_plane(lambda i, j: mine, lambda i, j: mine)
+    for copy in reversed(down_plane):
+        copy.wait_recv()
+    for i in range(X):
+        for h in BOTH:
+            for j in range(Y):
+                DS[h, 22 * j : 22 * j + 24, :] = YW[i * 4 + j, h].astype(f32)
+            WD[h, z, i] = DS[h, :88].astype(bf16)
+    down_z = Gather("z", lambda h, k: WD.at[h, at("z", k)])
+    down_z.start()
     for k in reversed(far):
         wide_z[k].wait_recv()
     for h in BOTH:
@@ -424,32 +446,40 @@
             for j in range(2):
                 parts = [WZ[4 * j + i, h].astype(f32)[rows] for i in range(4)]
                 WG[h, layer, x, y, 16 * j : 16 * j + 16, :] = jnp.concatenate(parts, 0).astype(bf16)
-    near = [Gather("y", lambda h, k: WG.at[h, 0, x, at("y", k)]), Gather("x", lambda h, k: WG.at[h, 1, at("x", k), y])]
+    near = [Gather("yx"[f], functools.partial(lambda f, h, k: unit(WG, f, h, 0, k), f)) for f in BOTH]
+    wide = [[Gather("xy"[f], functools.partial(lambda f, j, h, k: unit(WG, f, h, k, j), f, j)) for j in range(4)] for f in BOTH]
+
+    def spread(f, h, j):
+        for s in WAYS[:: 1 - 2 * h]:
+            wide[f][j % 4].push(h, s, 1)
+
+    def arrive_near(t, pair):
+        for f in BOTH:
+            for h, s in pair:
+                spread(f, h, near[f].arrive(h, s, t))
+
+    def arrive_wide(j, t, pair):
+        for f in BOTH:
+            for h, s in pair:
+                wide[f][j].arrive(h, s, t)
+
     for ring in near:
         ring.start()
-    arrive_pair(down_x, 1)
-    arrive_pair(down_x, 1, True)
-    arrive_pair(down_x, 2)
-    down_z = Gather("z", lambda h, k: WD.at[h, at("z", k)])
-    down_z.start()
-
-    for ring in near:
-        arrive_pair(ring, 1)
-    for ring in near:
-        arrive_pair(ring, 1, True)
-    far_rings = [Gather("x", lambda h, k: WG.at[h, 0, at("x", k)]), Gather("y", lambda h, k: WG.at[h, 1, :, at("y", k)])]
-    for f in BOTH:
-        arrive_pair(near[f], 2)
-        far_rings[f].start()
+    for f in BOTH:
+        for h in BOTH:
+            spread(f, h, 0)
+    arrive_near(1, LONG)
+    arrive_near(1, SHORT)
     arrive_pair(down_z, 1)
+    arrive_wide(0, 1, LONG)
+    arrive_near(2, LONG)
     arrive_pair(down_z, 1, True)
+    for j in (1, 3):
+        arrive_wide(j, 1, LONG)
     arrive_pair(down_z, 2)
-    for f in BOTH:
-        arrive_pair(far_rings[f], 1)
     arrive_pair(down_z, 2, True)
+    arrive_wide(2, 1, LONG)
     arrive_pair(down_z, 3)
-    for f in BOTH:
-        arrive_pair(far_rings[f], 1, True)
     arrive_pair(down_z, 3, True)
     arrive_pair(down_z, 4)
 
@@ -461,10 +491,12 @@
                 OD[layer, pl.ds(pl.multiple_of(i * 352, 32), 352), 256 * h : 256 * h + 256] = out[352 * layer : 352 * layer + 352]
 
     loop(4, restore)
-    for f in BOTH:
-        arrive_pair(far_rings[f], 2)
+    for j in range(4):
+        arrive_wide(j, 1, SHORT)
+        arrive_wide(j, 2, LONG)
     for copy in pending:
         copy.wait_send()
+    told.wait_send()
 
 
 def finish(W, OD, MW, MD, *rest):
@@ -482,7 +514,7 @@
     wide, deep = (2, 4, F), (11, 2, 512)
     unit, half = (4, 32, F), (4, 88, 256)
     pair, square, whole_down = (2, 2), (4, *unit), (2, 8, *half)
-    blocks, small, tile = (8, 2, 8, F), (4, 2, 24, 256), (8, 128)
+    blocks, small = (8, 2, 8, F), (16, 2, 24, 256)
     shape = jax.ShapeDtypeStruct
     out = pl.pallas_call(
         kernel,
@@ -493,7 +525,7 @@
             pltpu.VMEM((*pair, *square), bf16),
             pltpu.VMEM((2, F, 512), bf16),
             pltpu.VMEM(whole_down, bf16),
-            pltpu.VMEM((2, 6, *unit), bf16),
+            pltpu.VMEM((2, 4, 6, *unit[1:]), bf16),
             pltpu.VMEM((*pair, *unit), f32),
             pltpu.VMEM((*pair, *unit), bf16),
             pltpu.VMEM((2, 6, *unit[1:]), bf16),
@@ -502,15 +534,12 @@
             pltpu.VMEM(blocks, f32),
             pltpu.VMEM(blocks, bf16),
             pltpu.VMEM((14, *half), bf16),
-            pltpu.VMEM((2, *half), f32),
-            pltpu.VMEM((2, *half), bf16),
-            pltpu.VMEM((6, *half[1:]), bf16),
             pltpu.VMEM((2, 96, 256), f32),
             pltpu.VMEM(small, bf16),
             pltpu.VMEM(small, f32),
             pltpu.VMEM(small, bf16),
-            pltpu.VMEM((3, *tile), f32),
-            pltpu.VMEM((3, 8, *tile), f32),
+            pltpu.VMEM((1, 128), f32),
+            pltpu.VMEM((128, 1, 128), f32),
             pltpu.VMEM(whole_down, bf16),
             pltpu.VMEM(blocks, bf16),
             pltpu.VMEM(small, bf16),
@@ -524,6 +553,7 @@
             pltpu.SemaphoreType.DMA((SEMS,)),
             pltpu.SemaphoreType.DMA((LOADS,)),
             pltpu.SemaphoreType.DMA((9,)),
+            pltpu.SemaphoreType.DMA((2,)),
         ],
         compiler_params=pltpu.CompilerParams(collective_id=0, has_side_effects=True, vmem_limit_bytes=50 * 2**20),
         name="clipped_step",

time: 119 us -> 112 us (0.941)
  Pallas kernels: 118 us -> 112 us
    pallas_call x1, Pallas kernels: 115 us -> 108 us  [step_kernel(): pl.pallas_call(kernel, out_shape=(pltpu.VMEM((*pair, *square), bf16), plt...]
where the time goes in v4:
time: 112 us
  Pallas kernels  112 us (100%)
    pallas_call x1, Pallas kernels, step_kernel(): pl.pallas_call(kernel, out_shape=(pltpu.VMEM((*pair, *square), bf16), plt...  108 us
    pallas_call x1, Pallas kernels, step_kernel(): pl.pallas_call(finish, out_shape=(shape((2, *square), bf16),) * 2 + (shap...  3.57 us

profile of v4, /device:TPU:2, one launch (start us, length us, event | category | flops | bytes accessed | tf_op | source)
XLA Modules:
  0.0 112.3 jit_solution(13231147624049304243)
XLA Ops:
  0.6 108.1 %clipped_step.1 = (bf16[2,2,4,4,32,1408]{5,4,3,2,1,0:T(8,128)(2,1)S(1)}, bf16[2,1408,512]{2,1,0:T(8,128)(2,1)S(1)}, f32[2,2,2,4,1408]{4,3,2,1,0:T(4,128)S(1)}, f32[2,11,2,512]{3,2,1,0:T(2,128)S(1)}) custom-call(bf16[2,4,4,32,1408]{4,3,2,1,0:T(8,128)(2,1)} %bitcast.9, bf16[2,4,4,32,1408]{4,3,2,1,0:T(8,128)(2,1)} %bitcast.10, bf16[2,1408,512]{2,1,0:T(8,128)(2,1)} %bitcast.11, ...), custom_call_target="tpu_custom_call" | custom-call | tf_op jit(solution)/shard_map/clipped_step/pallas_call | solution.py:519
  108.8 3.6 %finish.1 = (bf16[2,4,4,32,1408]{4,3,2,1,0:T(8,128)(2,1)}, bf16[2,4,4,32,1408]{4,3,2,1,0:T(8,128)(2,1)}, bf16[2,1408,512]{2,1,0:T(8,128)(2,1)}, f32[2,4,1408]{2,...) custom-call(bf16[2,2,4,4,32,1408]{5,4,3,2,1,0:T(8,128)(2,1)S(1)} %ge, ...), custom_call_target="tpu_custom_call" | custom-call | tf_op jit(solution)/shard_map/finish/pallas_call | solution.py:562

commit v5 on v4

--- a/solution.py
+++ b/solution.py
@@ -2,6 +2,7 @@
 
 import jax
 import jax.numpy as jnp
+import numpy as np
 from jax import lax
 from jax.experimental import pallas as pl
 from jax.experimental.pallas import tpu as pltpu
@@ -10,7 +11,7 @@
 X, Y, Z = 4, 4, 8
 F = 1408
 COUNT = 3 * 2 * 512 * F
-SEMS = 256
+SEMS = 320
 LOADS = 32
 ROWS = 704
 f32, bf16 = jnp.float32, jnp.bfloat16
@@ -28,6 +29,12 @@
     return {key: i for i, key in enumerate((h, s, t) for h, s, length in chains(n) for t in range(1, length + 1))}
 
 
+def one_hots():
+    rows = np.arange(ROWS).reshape(2, 4, 8, 11).transpose(2, 1, 0, 3).reshape(-1)
+    forth = rows[:, None] == np.arange(ROWS)
+    return [jnp.asarray(p, bf16) for p in (forth, forth.T)]
+
+
 def loop(n, body):
     def step(i, carry):
         body(i)
@@ -36,9 +43,9 @@
     lax.fori_loop(0, n, step, 0)
 
 
-def kernel(gg, gu, gd, wg, wu, wd, mg, mu, md, vg, vu, vd, WG, OD, MW, MD, *scratch):
-    (G, GR, GD, L1, F1, B1, L2, F2, ZS, ZF, ZL, LZ, DS, YS, YF, YL, NS, NL, WD, WZ, YW, PF, PB, OW, OWD, IW, ID) = scratch[:-5]
-    ssem, rsem, lsem, wsem, nsem = scratch[-5:]
+def kernel(pf, pb, gg, gu, gd, wg, wu, wd, mg, mu, md, vg, vu, vd, WG, OD, MW, MD, *scratch):
+    (G, GR, GD, L1, F1, B1, L2, F2, ZS, ZF, ZL, LZ, DS, YS, YF, YL, NS, NL, WD, WZ, YW, PF, PB, OW, OWD, IW, ID) = scratch[:-4]
+    ssem, rsem, lsem, wsem = scratch[-4:]
     d = lax.axis_index("dp")
     x, y, z = d // 32, (d // 8) % 4, d % 8
     place = {"x": (x, 4), "y": (y, 4), "z": (z, 8)}
@@ -50,6 +57,11 @@
     def device(axis, k):
         p = at(axis, k)
         return {"x": p * 32 + y * 8 + z, "y": x * 32 + p * 8 + z, "z": x * 32 + y * 8 + p}[axis]
+
+    barrier = pltpu.get_barrier_semaphore()
+    for axis in place:
+        for way in WAYS:
+            pl.semaphore_signal(barrier, inc=1, device_id={"dp": device(axis, way)}, device_id_type=pl.DeviceIdType.MESH)
 
     used = [0]
     pending = []
@@ -68,10 +80,9 @@
     def send(src, dst, axis, k):
         return send_to(device(axis, k), src, dst)
 
-    plane = sorted(((i, j) for i in range(X) for j in range(Y) if i or j), key=lambda o: -sum(min(k, X - k) for k in o))
-
-    def send_plane(source, target):
-        return [send_to(at("x", i) * 32 + at("y", j) * 8 + z, source(i, j), target(i, j)) for i, j in plane]
+    def send_plane(i, source, target):
+        ks = [k for k in (2, 1, 3, 0) if i or k]
+        return {(i, k): send_to(at("x", i) * 32 + at("y", k) * 8 + z, source(k), target(k)) for k in ks}
 
     loads = {}
 
@@ -145,11 +156,13 @@
     for h in BOTH:
         for f in BOTH:
             load_wide(f, h, 2)
+    load(("down", 2), pf, PF)
     for i in BOTH:
         load(("down", i), gd.at[i], GR.at[i])
     for h, k in ((1, 1), (0, 3), (0, 1), (1, 3), (0, 0), (1, 0)):
         for f in BOTH:
             load_wide(f, h, k)
+    load(("back", 0), pb, PB)
     mine = pl.multiple_of(8 * (d // 2), 8)
     low = pl.multiple_of(8 * ((11 * d) // 8) - 8 * (d // 127), 8)
     own_w = [pltpu.make_async_copy(w.at[:, pl.ds(mine, 8), :], OW.at[i], wsem.at[i]) for i, w in enumerate((wg, wu))]
@@ -171,27 +184,6 @@
 
         return wait
 
-    barrier = pltpu.get_barrier_semaphore()
-    for axis in place:
-        for way in WAYS:
-            pl.semaphore_signal(barrier, inc=1, device_id={"dp": device(axis, way)}, device_id_type=pl.DeviceIdType.MESH)
-
-    row = lax.broadcasted_iota(jnp.int32, (ROWS, 128), 0)
-    lane = lax.broadcasted_iota(jnp.int32, (ROWS, 128), 1)
-
-    def split(i, n):
-        q = (i * (2**18 // n + 1)) >> 18
-        return q, i - q * n
-
-    def one_hot(ref, there):
-        for c in range(0, ROWS, 128):
-            n = min(128, ROWS - c)
-            ref[:, c : c + n] = jnp.where(there == lane + c, 1.0, 0.0).astype(bf16)[:, :n]
-
-    zz, rest = split(row, 88)
-    yy, rest = split(rest, 22)
-    layer, r = split(rest, 11)
-    one_hot(PF, layer * 352 + yy * 88 + zz * 11 + r)
     pl.semaphore_wait(barrier, 2 * len(place))
 
     def unit(ref, f, h, k, j):
@@ -230,28 +222,28 @@
 
             by_rows(body)
 
-    def add_down(got, h, k):
-        own = GD.at[h, at("z", k)]
-
-        def body(i):
-            got[i] = (got[i].astype(f32) + own[i].astype(f32)).astype(bf16)
-
-        loop(4, body)
-
-    down = Scatter("z", lambda h, k: GD.at[h, at("z", k)], LZ, add_down)
-
-    def end_down(h):
-        a, b = down.last(h)
-        own = GD.at[h, at("z", 0)]
-
-        def body(i):
-            DS[h, :88] = own[i].astype(f32) + a[i].astype(f32) + b[i].astype(f32)
-            for j in range(4):
-                block = DS[h, 22 * j : 22 * j + 24, :]
-                YF[i * 4 + j, h] = block
-                YS[i * 4 + j, h] = block.astype(bf16)
-
-        loop(4, body)
+    def down_stage(j):
+        def own(h, k):
+            return GD.at[h, at("z", k), at("x", j)]
+
+        def add(got, h, k):
+            got[...] = (got[...].astype(f32) + own(h, k)[...].astype(f32)).astype(bf16)
+
+        return Scatter("z", own, LZ.at[j], add)
+
+    down = [down_stage(j) for j in range(X)]
+
+    def end_down(j):
+        i = at("x", j)
+        for h in BOTH:
+            a, b = down[j].last(h)
+            DS[h, :88] = GD[h, z, i].astype(f32) + a[...].astype(f32) + b[...].astype(f32)
+            for yy in range(Y):
+                block = DS[h, 22 * yy : 22 * yy + 24, :]
+                YS[i * 4 + yy, h] = block.astype(bf16)
+                if j == 0:
+                    YF[yy, h] = block
+        return send_plane(j, lambda k: YS.at[i * 4 + at("y", k)], lambda k: YL.at[j * 4 + k])
 
     def second_stage(f):
         axis = "yx"[f]
@@ -289,85 +281,86 @@
     def arrive_first(j):
         for f in BOTH:
             arrive_pair(first[f][j], 1)
+
+    def arrive_down(t, short=False):
+        for j in order:
+            arrive_pair(down[j], t, short)
 
     order = (2, 1, 3, 0)
     for j in order:
         begin(j, LONG)
     for j in order[:2]:
         begin(j, SHORT)
-    for i in BOTH:
+    for i in range(3):
         loads["down", i].wait()
 
-    def permute(i):
+    def permute(j):
+        i = at("x", j)
         rows = GR[:, pl.ds(pl.multiple_of(i * 352, 32), 352), :].reshape(ROWS, 512)
         out = jnp.dot(PF[...], rows, preferred_element_type=f32)
         for zz in range(Z):
             for h in BOTH:
                 GD[h, zz, i] = out[88 * zz : 88 * zz + 88, 256 * h : 256 * h + 256].astype(bf16)
 
-    loop(4, permute)
-    down.start()
+    for j in order:
+        permute(j)
+        down[j].start()
     for j, later in zip(order, order[2:]):
         arrive_first(j)
         begin(later, SHORT)
     arrive_first(3)
-    arrive_pair(down, 1)
-    layer, rest = split(row, 352)
-    yy, rest = split(rest, 88)
-    zz, r = split(rest, 11)
-    one_hot(PB, zz * 88 + yy * 22 + layer * 11 + r)
+    arrive_down(1)
     for h in BOTH:
         DS[h, 88:] = jnp.zeros((8, 256), f32)
-    arrive_pair(down, 1, True)
+    arrive_down(1, True)
     for f in BOTH:
         end_first(f, 2)
         for h, s in LONG:
             second[f].first(h, s)
     arrive_first(0)
-    arrive_pair(down, 2)
+    arrive_down(2)
     for f in BOTH:
         end_first(f, 1)
-    arrive_pair(down, 2, True)
+    arrive_down(2, True)
     for f in BOTH:
         end_first(f, 3)
         for h, s in SHORT:
             second[f].first(h, s)
-    arrive_pair(down, 3)
+    arrive_down(3)
     for f in BOTH:
         arrive_pair(second[f], 1)
     for f in BOTH:
         end_first(f, 0)
-    for f in BOTH:
-        for h in BOTH:
+    far = (4, 3, 5, 2, 6, 1, 7)
+    third = []
+    for h in BOTH:
+        for f in BOTH:
             end_second(f, h)
-
-    for h in BOTH:
         for j in range(4):
             t0, t1 = (F2[f, h, 8 * j : 8 * j + 8, :] for f in BOTH)
             for i, block in enumerate((jnp.concatenate([t0[:4], t1[:4]], 0), jnp.concatenate([t0[4:], t1[4:]], 0))):
                 ZF[2 * j + i, h] = block
                 ZS[2 * j + i, h] = block.astype(bf16)
-    far = (4, 3, 5, 2, 6, 1, 7)
-    third = {k: send(ZS.at[at("z", k)], ZL.at[k], "z", k) for k in far}
-    for h in BOTH:
-        end_down(h)
-    third_down = send_plane(lambda i, j: YS.at[at("x", i) * 4 + at("y", j)], lambda i, j: YL.at[i * 4 + j])
-    for copy in reversed(third_down):
+        third.append({k: send(ZS.at[at("z", k), h], ZL.at[k, h], "z", k) for k in far})
+    third_down = {}
+    for j in order:
+        third_down.update(end_down(j))
+    for copy in third_down.values():
         copy.wait_recv()
     real = lax.broadcasted_iota(jnp.int32, (24, 256), 0) < 22
     squares = jnp.zeros((), f32)
     g_down = []
     for h in BOTH:
-        total = YF[x * 4 + y, h]
+        total = YF[y, h]
         for k in range(1, 16):
             total = total + YL[k, h].astype(f32)
         total = jnp.where(real, total, 0.0).astype(bf16).astype(f32)
         g_down.append(total)
         squares += jnp.sum(total * total)
-    for k in reversed(far):
-        third[k].wait_recv()
     g_wide = []
     for h in BOTH:
+        for k in reversed(far):
+            third[h][k].wait_recv()
         total = ZF[z, h]
         for k in range(1, 8):
             total = total + ZL[k, h].astype(f32)
@@ -375,24 +368,21 @@
         g_wide.append(total)
         squares += jnp.sum(total * total)
 
-    NS[...] = jnp.full((1, 128), squares, f32)
-    NL[0] = NS[...]
-
-    def norm_copy(src, dst, target):
-        return pltpu.make_async_remote_copy(
-            src_ref=src, dst_ref=dst, send_sem=nsem.at[0], recv_sem=nsem.at[1],
-            device_id={"dp": target}, device_id_type=pl.DeviceIdType.MESH,
-        )
-
-    def tell(i):
-        k = lax.rem(i + 63, 127) + 1
-        norm_copy(NS, NL.at[k], lax.rem(d + k, 128)).start()
-
-    loop(127, tell)
-    others = NL.at[pl.ds(1, 127)]
-    told = norm_copy(others, others, device("x", 1))
-    told.wait_recv()
-    total = jnp.sum(NL[...], axis=0)
+    total = jnp.full((1, 128), squares, f32)
+    NS[0] = total
+    told = {}
+    for i in order:
+        told.update(send_plane(i, lambda k: NS.at[0], lambda k: NL.at[i * 4 + k]))
+    for copy in told.values():
+        copy.wait_recv()
+    for k in range(1, 16):
+        total = total + NL[k]
+    NS[1] = total
+    told = {k: send(NS.at[1], NL.at[16 + k], "z", k) for k in far}
+    for k in reversed(far):
+        told[k].wait_recv()
+    for k in range(1, 8):
+        total = total + NL[16 + k]
     factor = jnp.minimum(1.0, 0.5 * lax.rsqrt(total / COUNT + 1e-30))[0:1, 0:1]
 
     def adamw(w, m, v, g):
@@ -426,26 +416,33 @@
     for h in BOTH:
         YW[x * 4 + y, h] = DS[h, :24].astype(bf16)
 
-    wide_z = {k: send(WZ.at[z], WZ.at[z], "z", k) for k in far}
+    wide_z = [{k: send(WZ.at[z, h], WZ.at[z, h], "z", k) for k in far} for h in BOTH]
     mine = YW.at[x * 4 + y]
-    down_plane = send_plane(lambda i, j: mine, lambda i, j: mine)
-    for copy in reversed(down_plane):
-        copy.wait_recv()
-    for i in range(X):
+    plane = {}
+    for i in (0, 2, 1, 3):
+        plane.update(send_plane(i, lambda k: mine, lambda k: mine))
+    down = [Gather("z", functools.partial(lambda j, h, k: WD.at[h, at("z", k), at("x", j)], j)) for j in range(X)]
+
+    def begin_down(j):
+        for k in range(Y):
+            if (j, k) != (0, 0):
+                plane[-j % 4, k].wait_recv()
+        i = at("x", j)
         for h in BOTH:
-            for j in range(Y):
-                DS[h, 22 * j : 22 * j + 24, :] = YW[i * 4 + j, h].astype(f32)
+            for yy in range(Y):
+                DS[h, 22 * yy : 22 * yy + 24, :] = YW[i * 4 + yy, h].astype(f32)
             WD[h, z, i] = DS[h, :88].astype(bf16)
-    down_z = Gather("z", lambda h, k: WD.at[h, at("z", k)])
-    down_z.start()
-    for k in reversed(far):
-        wide_z[k].wait_recv()
-    for h in BOTH:
+        down[j].start()
+
+    def begin_wide(h):
+        for k in reversed(far):
+            wide_z[h][k].wait_recv()
         for layer in BOTH:
             rows = slice(4 * layer, 4 * layer + 4)
             for j in range(2):
                 parts = [WZ[4 * j + i, h].astype(f32)[rows] for i in range(4)]
                 WG[h, layer, x, y, 16 * j : 16 * j + 16, :] = jnp.concatenate(parts, 0).astype(bf16)
+
     near = [Gather("yx"[f], functools.partial(lambda f, h, k: unit(WG, f, h, 0, k), f)) for f in BOTH]
     wide = [[Gather("xy"[f], functools.partial(lambda f, j, h, k: unit(WG, f, h, k, j), f, j)) for j in range(4)] for f in BOTH]
 
@@ -463,40 +460,43 @@
             for h, s in pair:
                 wide[f][j].arrive(h, s, t)
 
-    for ring in near:
-        ring.start()
-    for f in BOTH:
-        for h in BOTH:
+    begin_down(0)
+    for h in BOTH:
+        begin_wide(h)
+        for f in BOTH:
+            for s in WAYS[:: 1 - 2 * h]:
+                near[f].push(h, s, 1)
+        for f in BOTH:
             spread(f, h, 0)
+        if h == 0:
+            for j in order[:3]:
+                begin_down(j)
     arrive_near(1, LONG)
     arrive_near(1, SHORT)
-    arrive_pair(down_z, 1)
+    arrive_down(1)
     arrive_wide(0, 1, LONG)
     arrive_near(2, LONG)
-    arrive_pair(down_z, 1, True)
+    arrive_down(1, True)
     for j in (1, 3):
         arrive_wide(j, 1, LONG)
-    arrive_pair(down_z, 2)
-    arrive_pair(down_z, 2, True)
+    arrive_down(2)
+    arrive_down(2, True)
     arrive_wide(2, 1, LONG)
-    arrive_pair(down_z, 3)
-    arrive_pair(down_z, 3, True)
-    arrive_pair(down_z, 4)
-
-    def restore(i):
+    arrive_down(3)
+    loads["back", 0].wait()
+    for j in (0, 2, 1, 3):
+        arrive_pair(down[j], 3, True)
+        arrive_pair(down[j], 4)
+        i = at("x", j)
         for h in BOTH:
             rows = WD[h, :, i].astype(f32).reshape(ROWS, 256).astype(bf16)
             out = jnp.dot(PB[...], rows, preferred_element_type=f32).astype(bf16)
             for layer in BOTH:
                 OD[layer, pl.ds(pl.multiple_of(i * 352, 32), 352), 256 * h : 256 * h + 256] = out[352 * layer : 352 * layer + 352]
-
-    loop(4, restore)
-    for j in range(4):
         arrive_wide(j, 1, SHORT)
         arrive_wide(j, 2, LONG)
     for copy in pending:
         copy.wait_send()
-    told.wait_send()
 
 
 def finish(W, OD, MW, MD, *rest):
@@ -519,7 +519,7 @@
     out = pl.pallas_call(
         kernel,
         out_shape=(pltpu.VMEM((*pair, *square), bf16), pltpu.VMEM((2, F, 512), bf16), pltpu.VMEM((*pair, *wide), f32), pltpu.VMEM((2, *deep), f32)),
-        in_specs=[hbm] * 12,
+        in_specs=[hbm] * 14,
         out_specs=(vmem,) * 4,
         scratch_shapes=[
             pltpu.VMEM((*pair, *square), bf16),
@@ -533,13 +533,13 @@
             pltpu.VMEM(blocks, bf16),
             pltpu.VMEM(blocks, f32),
             pltpu.VMEM(blocks, bf16),
-            pltpu.VMEM((14, *half), bf16),
+            pltpu.VMEM((4, 14, *half[1:]), bf16),
             pltpu.VMEM((2, 96, 256), f32),
             pltpu.VMEM(small, bf16),
-            pltpu.VMEM(small, f32),
+            pltpu.VMEM((4, *small[1:]), f32),
             pltpu.VMEM(small, bf16),
-            pltpu.VMEM((1, 128), f32),
-            pltpu.VMEM((128, 1, 128), f32),
+            pltpu.VMEM((2, 1, 128), f32),
+            pltpu.VMEM((24, 1, 128), f32),
             pltpu.VMEM(whole_down, bf16),
             pltpu.VMEM(blocks, bf16),
             pltpu.VMEM(small, bf16),
@@ -553,11 +553,10 @@
             pltpu.SemaphoreType.DMA((SEMS,)),
             pltpu.SemaphoreType.DMA((LOADS,)),
             pltpu.SemaphoreType.DMA((9,)),
-            pltpu.SemaphoreType.DMA((2,)),
         ],
         compiler_params=pltpu.CompilerParams(collective_id=0, has_side_effects=True, vmem_limit_bytes=50 * 2**20),
         name="clipped_step",
-    )(*args)
+    )(*one_hots(), *args)
     out = [pltpu.with_memory_space_constraint(one, pltpu.VMEM) for one in out]
     return pl.pallas_call(
         finish,

time: 112 us -> 109 us (0.973); the launches traced: 112 us -> 108 us
  Pallas kernels: 112 us -> 107 us
    pallas_call x1, Pallas kernels: 108 us -> 104 us  [step_kernel(): pl.pallas_call(kernel, out_shape=(pltpu.VMEM((*pair, *square), bf16), plt...]
where the time goes in v5:
time: 109 us; the launch traced here: 108 us
  Pallas kernels  107 us (98%)
    pallas_call x1, Pallas kernels, step_kernel(): pl.pallas_call(kernel, out_shape=(pltpu.VMEM((*pair, *square), bf16), plt...  104 us
    pallas_call x1, Pallas kernels, step_kernel(): pl.pallas_call(finish, out_shape=(shape((2, *square), bf16),) * 2 + (shap...  3.57 us

profile of v5, /device:TPU:2, one launch (start us, length us, event | category | flops | bytes accessed | tf_op | source)
XLA Modules:
  0.0 107.8 jit_solution(17487282380390181093)
XLA Ops:
  0.6 103.6 %clipped_step.1 = (bf16[2,2,4,4,32,1408]{5,4,3,2,1,0:T(8,128)(2,1)S(1)}, bf16[2,1408,512]{2,1,0:T(8,128)(2,1)S(1)}, f32[2,2,2,4,1408]{4,3,2,1,0:T(4,128)S(1)}, f32[2,11,2,512]{3,2,1,0:T(2,128)S(1)}) custom-call(bf16[704,704]{1,0:T(8,128)(2,1)} %constant.4.clone.pf, bf16[704,704]{1,0:T(8,128)(2,1)} %constant.5.clone.pb, bf16[2,4,4,32,1408]{4,3,2,1,0:T(8,128)(2,1)} %bitcast.9, ...), custom_call_target="tpu_custom_call" | custom-call | tf_op jit(solution)/shard_map/clipped_step/pallas_call | solution.py:519
  104.3 3.6 %finish.1 = (bf16[2,4,4,32,1408]{4,3,2,1,0:T(8,128)(2,1)}, bf16[2,4,4,32,1408]{4,3,2,1,0:T(8,128)(2,1)}, bf16[2,1408,512]{2,1,0:T(8,128)(2,1)}, f32[2,4,1408]{2,...) custom-call(bf16[2,2,4,4,32,1408]{5,4,3,2,1,0:T(8,128)(2,1)S(1)} %ge, ...), custom_call_target="tpu_custom_call" | custom-call | tf_op jit(solution)/shard_map/finish/pallas_call | solution.py:561

commit v6 on v5

--- a/solution.py
+++ b/solution.py
@@ -153,26 +153,30 @@
         else:
             load((f, h, k), (gg, gu)[h].at[1, :, at("y", k)], G.at[h, 1, :, at("y", k)])
 
-    for h in BOTH:
-        for f in BOTH:
-            load_wide(f, h, 2)
+    for h, k in ((0, 2), (1, 2), (1, 1), (0, 3)):
+        for f in BOTH:
+            load_wide(f, h, k)
     load(("down", 2), pf, PF)
     for i in BOTH:
         load(("down", i), gd.at[i], GR.at[i])
-    for h, k in ((1, 1), (0, 3), (0, 1), (1, 3), (0, 0), (1, 0)):
-        for f in BOTH:
-            load_wide(f, h, k)
-    load(("back", 0), pb, PB)
-    mine = pl.multiple_of(8 * (d // 2), 8)
     low = pl.multiple_of(8 * ((11 * d) // 8) - 8 * (d // 127), 8)
-    own_w = [pltpu.make_async_copy(w.at[:, pl.ds(mine, 8), :], OW.at[i], wsem.at[i]) for i, w in enumerate((wg, wu))]
-    own_w.append(pltpu.make_async_copy(wd.at[:, pl.ds(low, 24), :], OWD, wsem.at[2]))
-    for i, (wide_, deep_) in enumerate((((mg, mu), md), ((vg, vu), vd))):
-        for h in BOTH:
-            own_w.append(pltpu.make_async_copy(wide_[h], IW.at[i, h], wsem.at[len(own_w)]))
-        own_w.append(pltpu.make_async_copy(deep_, ID.at[i], wsem.at[len(own_w)]))
-    for copy in own_w:
-        copy.start()
+    own_w = []
+
+    def load_rest():
+        for h, k in ((0, 1), (1, 3), (0, 0), (1, 0)):
+            for f in BOTH:
+                load_wide(f, h, k)
+        load(("back", 0), pb, PB)
+        mine = pl.multiple_of(8 * (d // 2), 8)
+        pairs = [(w.at[:, pl.ds(mine, 8), :], OW.at[i]) for i, w in enumerate((wg, wu))]
+        pairs.append((wd.at[:, pl.ds(low, 24), :], OWD))
+        for i, (wide_, deep_) in enumerate((((mg, mu), md), ((vg, vu), vd))):
+            pairs += [(wide_[h], IW.at[i, h]) for h in BOTH]
+            pairs.append((deep_, ID.at[i]))
+        for src, dst in pairs:
+            own_w.append(pltpu.make_async_copy(src, dst, wsem.at[len(own_w)]))
+            own_w[-1].start()
+
     ready = set()
 
     def need(f, n):
@@ -291,6 +295,7 @@
         begin(j, LONG)
     for j in order[:2]:
         begin(j, SHORT)
+    load_rest()
     for i in range(3):
         loads["down", i].wait()
 
@@ -393,11 +398,13 @@
     for copy in own_w:
         copy.wait()
     odd = d % 2 == 1
+    wide_z = []
     for h in BOTH:
         w = [OW[h, i].astype(f32) for i in BOTH]
         w = jnp.concatenate([jnp.where(odd, one[4:], one[:4]) for one in w], 0)
         m, v = (jnp.concatenate([IW[i, h, 0], IW[i, h, 1]], 0) for i in BOTH)
         WZ[z, h], *new = adamw(w, m, v, g_wide[h] * factor)
+        wide_z.append({k: send(WZ.at[z, h], WZ.at[z, h], "z", k) for k in far})
         for i, one in enumerate(new):
             for layer in BOTH:
                 MW[i, h, layer] = one[4 * layer : 4 * layer + 4]
@@ -416,7 +423,6 @@
     for h in BOTH:
         YW[x * 4 + y, h] = DS[h, :24].astype(bf16)
 
-    wide_z = [{k: send(WZ.at[z, h], WZ.at[z, h], "z", k) for k in far} for h in BOTH]
     mine = YW.at[x * 4 + y]
     plane = {}
     for i in (0, 2, 1, 3):

time: 109 us -> 108 us (level)
  no operation moved by 1% of the time
where the time goes in v6:
time: 108 us; the launch traced here: 107 us
  Pallas kernels  107 us (99%)
    pallas_call x1, Pallas kernels, step_kernel(): pl.pallas_call(kernel, out_shape=(pltpu.VMEM((*pair, *square), bf16), plt...  103 us
    pallas_call x1, Pallas kernels, step_kernel(): pl.pallas_call(finish, out_shape=(shape((2, *square), bf16),) * 2 + (shap...  3.57 us

profile of v6, /device:TPU:2, one launch (start us, length us, event | category | flops | bytes accessed | tf_op | source)
XLA Modules:
  0.0 107.2 jit_solution(4393049381003882468)
XLA Ops:
  0.6 103.0 %clipped_step.1 = (bf16[2,2,4,4,32,1408]{5,4,3,2,1,0:T(8,128)(2,1)S(1)}, bf16[2,1408,512]{2,1,0:T(8,128)(2,1)S(1)}, f32[2,2,2,4,1408]{4,3,2,1,0:T(4,128)S(1)}, f32[2,11,2,512]{3,2,1,0:T(2,128)S(1)}) custom-call(bf16[704,704]{1,0:T(8,128)(2,1)} %constant.4.clone.pf, bf16[704,704]{1,0:T(8,128)(2,1)} %constant.5.clone.pb, bf16[2,4,4,32,1408]{4,3,2,1,0:T(8,128)(2,1)} %bitcast.9, ...), custom_call_target="tpu_custom_call" | custom-call | tf_op jit(solution)/shard_map/clipped_step/pallas_call | solution.py:525
  103.7 3.6 %finish.1 = (bf16[2,4,4,32,1408]{4,3,2,1,0:T(8,128)(2,1)}, bf16[2,4,4,32,1408]{4,3,2,1,0:T(8,128)(2,1)}, bf16[2,1408,512]{2,1,0:T(8,128)(2,1)}, f32[2,4,1408]{2,...) custom-call(bf16[2,2,4,4,32,1408]{5,4,3,2,1,0:T(8,128)(2,1)S(1)} %ge, ...), custom_call_target="tpu_custom_call" | custom-call | tf_op jit(solution)/shard_map/finish/pallas_call | solution.py:567

commit v7 on v6

--- a/solution.py
+++ b/solution.py
@@ -337,7 +337,7 @@
     for f in BOTH:
         end_first(f, 0)
     far = (4, 3, 5, 2, 6, 1, 7)
-    third = []
+    third, relay = [], []
     for h in BOTH:
         for f in BOTH:
             end_second(f, h)
@@ -346,7 +346,14 @@
             for i, block in enumerate((jnp.concatenate([t0[:4], t1[:4]], 0), jnp.concatenate([t0[4:], t1[4:]], 0))):
                 ZF[2 * j + i, h] = block
                 ZS[2 * j + i, h] = block.astype(bf16)
-        third.append({k: send(ZS.at[at("z", k), h], ZL.at[k, h], "z", k) for k in far})
+        way = WAYS[h]
+        relay.append(send(ZS.at[at("z", 4), h], ZL.at[4, h], "z", way))
+        third.append({k: send(ZS.at[at("z", k), h], ZL.at[k, h], "z", k) for k in (-3 * way % Z, 2, 6)})
+    for h in BOTH:
+        k = 3 * WAYS[h] % Z
+        relay[h].wait_recv()
+        ZL[4, h] = (ZL[4, h].astype(f32) + ZF[at("z", k), h]).astype(bf16)
+        third[h].update({k: send(src, ZL.at[k, h], "z", k) for k, src in ((k, ZL.at[4, h]), (1, ZS.at[at("z", 1), h]), (7, ZS.at[at("z", 7), h]))})
     third_down = {}
     for j in order:
         third_down.update(end_down(j))
@@ -364,10 +371,10 @@
         squares += jnp.sum(total * total)
     g_wide = []
     for h in BOTH:
-        for k in reversed(far):
-            third[h][k].wait_recv()
+        for copy in third[h].values():
+            copy.wait_recv()
         total = ZF[z, h]
-        for k in range(1, 8):
+        for k in third[h]:
             total = total + ZL[k, h].astype(f32)
         total = total.astype(bf16).astype(f32)
         g_wide.append(total)
@@ -404,7 +411,7 @@
         w = jnp.concatenate([jnp.where(odd, one[4:], one[:4]) for one in w], 0)
         m, v = (jnp.concatenate([IW[i, h, 0], IW[i, h, 1]], 0) for i in BOTH)
         WZ[z, h], *new = adamw(w, m, v, g_wide[h] * factor)
-        wide_z.append({k: send(WZ.at[z, h], WZ.at[z, h], "z", k) for k in far})
+        wide_z.append({k: send(WZ.at[z, h], WZ.at[z, h], "z", k) for k in (3, 5, 2, 6, 1, 7)})
         for i, one in enumerate(new):
             for layer in BOTH:
                 MW[i, h, layer] = one[4 * layer : 4 * layer + 4]
@@ -425,7 +432,8 @@
 
     mine = YW.at[x * 4 + y]
     plane = {}
-    for i in (0, 2, 1, 3):
+    spread_order = (0, 2, 1, 3)
+    for i in spread_order:
         plane.update(send_plane(i, lambda k: mine, lambda k: mine))
     down = [Gather("z", functools.partial(lambda j, h, k: WD.at[h, at("z", k), at("x", j)], j)) for j in range(X)]
 
@@ -441,8 +449,8 @@
         down[j].start()
 
     def begin_wide(h):
-        for k in reversed(far):
-            wide_z[h][k].wait_recv()
+        for copy in wide_z[h].values():
+            copy.wait_recv()
         for layer in BOTH:
             rows = slice(4 * layer, 4 * layer + 4)
             for j in range(2):
@@ -456,16 +464,25 @@
         for s in WAYS[:: 1 - 2 * h]:
             wide[f][j % 4].push(h, s, 1)
 
-    def arrive_near(t, pair):
-        for f in BOTH:
-            for h, s in pair:
+    def arrive_near(h, t, ways=WAYS):
+        for s in ways:
+            for f in BOTH:
                 spread(f, h, near[f].arrive(h, s, t))
 
-    def arrive_wide(j, t, pair):
-        for f in BOTH:
-            for h, s in pair:
-                wide[f][j].arrive(h, s, t)
-
+    def arrive_wide(j, h, t=1):
+        for f in BOTH:
+            wide[f][j].arrive(h, WAYS[h], t)
+
+    def both_down(t, *js):
+        for j in js:
+            arrive_pair(down[j], t)
+            arrive_pair(down[j], t, True)
+
+    for h, way in enumerate(WAYS):
+        k = 3 * way % Z
+        wide_z[h].pop(k).wait_recv()
+        other = WZ.at[at("z", -k), h]
+        wide_z[h][4] = send(other, other, "z", way)
     begin_down(0)
     for h in BOTH:
         begin_wide(h)
@@ -477,20 +494,32 @@
         if h == 0:
             for j in order[:3]:
                 begin_down(j)
-    arrive_near(1, LONG)
-    arrive_near(1, SHORT)
-    arrive_down(1)
-    arrive_wide(0, 1, LONG)
-    arrive_near(2, LONG)
-    arrive_down(1, True)
-    for j in (1, 3):
-        arrive_wide(j, 1, LONG)
-    arrive_down(2)
-    arrive_down(2, True)
-    arrive_wide(2, 1, LONG)
-    arrive_down(3)
+    arrive_near(0, 1)
+    both_down(1, 0)
+    arrive_wide(0, 0)
+    both_down(1, 2)
+    arrive_near(1, 1)
+    both_down(1, 1)
+    arrive_wide(0, 1)
+    both_down(1, 3)
+    arrive_near(0, 2, WAYS[:1])
+    both_down(2, 0)
+    arrive_wide(3, 0)
+    both_down(2, 2)
+    arrive_wide(1, 0)
+    arrive_near(1, 2, WAYS[1:])
+    both_down(2, 1)
+    arrive_wide(1, 1)
+    both_down(2, 3)
+    arrive_wide(3, 1)
+    for j in spread_order[:2]:
+        arrive_pair(down[j], 3)
+    for h in BOTH:
+        arrive_wide(2, h)
+    for j in spread_order[2:]:
+        arrive_pair(down[j], 3)
     loads["back", 0].wait()
-    for j in (0, 2, 1, 3):
+    for j in spread_order:
         arrive_pair(down[j], 3, True)
         arrive_pair(down[j], 4)
         i = at("x", j)
@@ -499,8 +528,11 @@
             out = jnp.dot(PB[...], rows, preferred_element_type=f32).astype(bf16)
             for layer in BOTH:
                 OD[layer, pl.ds(pl.multiple_of(i * 352, 32), 352), 256 * h : 256 * h + 256] = out[352 * layer : 352 * layer + 352]
-        arrive_wide(j, 1, SHORT)
-        arrive_wide(j, 2, LONG)
+    for j in spread_order:
+        for f in BOTH:
+            arrive_pair(wide[f][j], 1, True)
+        for h in BOTH:
+            arrive_wide(j, h, 2)
     for copy in pending:
         copy.wait_send()
 

time: 108 us -> 107 us (level); the launches traced: 107 us -> 107 us
  no operation moved by 1% of the time
where the time goes in v7:
time: 107 us
  Pallas kernels  107 us (100%)
    pallas_call x1, Pallas kernels, step_kernel(): pl.pallas_call(kernel, out_shape=(pltpu.VMEM((*pair, *square), bf16), plt...  103 us
    pallas_call x1, Pallas kernels, step_kernel(): pl.pallas_call(finish, out_shape=(shape((2, *square), bf16),) * 2 + (shap...  3.57 us

profile of v7, /device:TPU:2, one launch (start us, length us, event | category | flops | bytes accessed | tf_op | source)
XLA Modules:
  0.0 107.3 jit_solution(605968280771737276)
XLA Ops:
  0.6 103.1 %clipped_step.1 = (bf16[2,2,4,4,32,1408]{5,4,3,2,1,0:T(8,128)(2,1)S(1)}, bf16[2,1408,512]{2,1,0:T(8,128)(2,1)S(1)}, f32[2,2,2,4,1408]{4,3,2,1,0:T(4,128)S(1)}, f32[2,11,2,512]{3,2,1,0:T(2,128)S(1)}) custom-call(bf16[704,704]{1,0:T(8,128)(2,1)} %constant.4.clone.pf, bf16[704,704]{1,0:T(8,128)(2,1)} %constant.5.clone.pb, bf16[2,4,4,32,1408]{4,3,2,1,0:T(8,128)(2,1)} %bitcast.9, ...), custom_call_target="tpu_custom_call" | custom-call | tf_op jit(solution)/shard_map/clipped_step/pallas_call | solution.py:557
  103.8 3.6 %finish.1 = (bf16[2,4,4,32,1408]{4,3,2,1,0:T(8,128)(2,1)}, bf16[2,4,4,32,1408]{4,3,2,1,0:T(8,128)(2,1)}, bf16[2,1408,512]{2,1,0:T(8,128)(2,1)}, f32[2,4,1408]{2,...) custom-call(bf16[2,2,4,4,32,1408]{5,4,3,2,1,0:T(8,128)(2,1)S(1)} %ge, ...), custom_call_target="tpu_custom_call" | custom-call | tf_op jit(solution)/shard_map/finish/pallas_call | solution.py:599

commit v8 on v7

--- a/solution.py
+++ b/solution.py
@@ -209,8 +209,8 @@
 
     first = [[first_stage(f, j) for j in range(4)] for f in BOTH]
 
-    def end_first(f, j):
-        for h in BOTH:
+    def end_first(h, j):
+        for f in BOTH:
             a, b = first[f][j].last(h)
             need(f, 4)(h, 0)
             own = unit(G, f, h, 0, j)
@@ -277,24 +277,36 @@
         for h, s in SHORT if short else LONG:
             ring.arrive(h, s, t)
 
-    def begin(j, pair):
-        for f in BOTH:
-            for h, s in pair:
-                first[f][j].first(h, s)
-
-    def arrive_first(j):
-        for f in BOTH:
-            arrive_pair(first[f][j], 1)
+    def begin(which, *js):
+        for j in js:
+            for f in BOTH:
+                first[f][j].first(*which)
+
+    def arrive_first(which, *js):
+        for j in js:
+            for f in BOTH:
+                first[f][j].arrive(*which, 1)
+
+    def begin_second(which):
+        for f in BOTH:
+            second[f].first(*which)
+
+    def arrive_second(which):
+        for f in BOTH:
+            second[f].arrive(*which, 1)
 
     def arrive_down(t, short=False):
         for j in order:
             arrive_pair(down[j], t, short)
 
+    gate_long, up_long = LONG
+    up_short, gate_short = SHORT
+    gate, up = BOTH
     order = (2, 1, 3, 0)
-    for j in order:
-        begin(j, LONG)
-    for j in order[:2]:
-        begin(j, SHORT)
+    u2, u1, u3, u0 = order
+    begin(gate_long, *order)
+    begin(gate_short, *order)
+    begin(up_long, *order)
     load_rest()
     for i in range(3):
         loads["down", i].wait()
@@ -310,35 +322,36 @@
     for j in order:
         permute(j)
         down[j].start()
-    for j, later in zip(order, order[2:]):
-        arrive_first(j)
-        begin(later, SHORT)
-    arrive_first(3)
+    arrive_first(gate_long, u2, u1, u3)
     arrive_down(1)
+    arrive_first(gate_long, u0)
     for h in BOTH:
         DS[h, 88:] = jnp.zeros((8, 256), f32)
+    end_first(gate, u2)
+    begin_second(gate_long)
     arrive_down(1, True)
-    for f in BOTH:
-        end_first(f, 2)
-        for h, s in LONG:
-            second[f].first(h, s)
-    arrive_first(0)
+    begin(up_short, u2, u1)
+    arrive_first(up_long, u2, u1)
+    end_first(gate, u1)
+    end_first(gate, u3)
+    begin_second(gate_short)
+    arrive_first(up_long, u3)
     arrive_down(2)
-    for f in BOTH:
-        end_first(f, 1)
+    end_first(gate, u0)
+    arrive_second(gate_long)
     arrive_down(2, True)
-    for f in BOTH:
-        end_first(f, 3)
-        for h, s in SHORT:
-            second[f].first(h, s)
+    begin(up_short, u3, u0)
+    end_first(up, u2)
+    begin_second(up_long)
+    arrive_first(up_long, u0)
+    end_first(up, u1)
+    begin_second(up_short)
     arrive_down(3)
-    for f in BOTH:
-        arrive_pair(second[f], 1)
-    for f in BOTH:
-        end_first(f, 0)
+
     far = (4, 3, 5, 2, 6, 1, 7)
-    third, relay = [], []
-    for h in BOTH:
+    third, relay, third_down = [], [], {}
+
+    def begin_third(h):
         for f in BOTH:
             end_second(f, h)
         for j in range(4):
@@ -349,14 +362,24 @@
         way = WAYS[h]
         relay.append(send(ZS.at[at("z", 4), h], ZL.at[4, h], "z", way))
         third.append({k: send(ZS.at[at("z", k), h], ZL.at[k, h], "z", k) for k in (-3 * way % Z, 2, 6)})
-    for h in BOTH:
+
+    def pass_on(h):
         k = 3 * WAYS[h] % Z
         relay[h].wait_recv()
         ZL[4, h] = (ZL[4, h].astype(f32) + ZF[at("z", k), h]).astype(bf16)
         third[h].update({k: send(src, ZL.at[k, h], "z", k) for k, src in ((k, ZL.at[4, h]), (1, ZS.at[at("z", 1), h]), (7, ZS.at[at("z", 7), h]))})
-    third_down = {}
-    for j in order:
+
+    begin_third(gate)
+    end_first(up, u3)
+    arrive_second(up_long)
+    third_down.update(end_down(u2))
+    end_first(up, u0)
+    for j in (u1, u3):
         third_down.update(end_down(j))
+    pass_on(gate)
+    third_down.update(end_down(u0))
+    begin_third(up)
+    pass_on(up)
     for copy in third_down.values():
         copy.wait_recv()
     real = lax.broadcasted_iota(jnp.int32, (24, 256), 0) < 22

time: 107 us -> 106 us (level); the launches traced: 107 us -> 105 us
  Pallas kernels: 107 us -> 104 us
    pallas_call x1, Pallas kernels: 103 us -> 100 us  [step_kernel(): pl.pallas_call(kernel, out_shape=(pltpu.VMEM((*pair, *square), bf16), plt...]
where the time goes in v8:
time: 106 us; the launch traced here: 105 us
  Pallas kernels  104 us (98%)
    pallas_call x1, Pallas kernels, step_kernel(): pl.pallas_call(kernel, out_shape=(pltpu.VMEM((*pair, *square), bf16), plt...  100 us
    pallas_call x1, Pallas kernels, step_kernel(): pl.pallas_call(finish, out_shape=(shape((2, *square), bf16),) * 2 + (shap...  3.57 us

profile of v8, /device:TPU:2, one launch (start us, length us, event | category | flops | bytes accessed | tf_op | source)
XLA Modules:
  0.0 104.6 jit_solution(18124175080376522510)
XLA Ops:
  0.6 100.4 %clipped_step.1 = (bf16[2,2,4,4,32,1408]{5,4,3,2,1,0:T(8,128)(2,1)S(1)}, bf16[2,1408,512]{2,1,0:T(8,128)(2,1)S(1)}, f32[2,2,2,4,1408]{4,3,2,1,0:T(4,128)S(1)}, f32[2,11,2,512]{3,2,1,0:T(2,128)S(1)}) custom-call(bf16[704,704]{1,0:T(8,128)(2,1)} %constant.4.clone.pf, bf16[704,704]{1,0:T(8,128)(2,1)} %constant.5.clone.pb, bf16[2,4,4,32,1408]{4,3,2,1,0:T(8,128)(2,1)} %bitcast.9, ...), custom_call_target="tpu_custom_call" | custom-call | tf_op jit(solution)/shard_map/clipped_step/pallas_call | solution.py:580
  101.0 3.6 %finish.1 = (bf16[2,4,4,32,1408]{4,3,2,1,0:T(8,128)(2,1)}, bf16[2,4,4,32,1408]{4,3,2,1,0:T(8,128)(2,1)}, bf16[2,1408,512]{2,1,0:T(8,128)(2,1)}, f32[2,4,1408]{2,...) custom-call(bf16[2,2,4,4,32,1408]{5,4,3,2,1,0:T(8,128)(2,1)S(1)} %ge, ...), custom_call_target="tpu_custom_call" | custom-call | tf_op jit(solution)/shard_map/finish/pallas_call | solution.py:622

commit v9 on v8

--- a/solution.py
+++ b/solution.py
@@ -349,7 +349,7 @@
     arrive_down(3)
 
     far = (4, 3, 5, 2, 6, 1, 7)
-    third, relay, third_down = [], [], {}
+    third, third_down = [], {}
 
     def begin_third(h):
         for f in BOTH:
@@ -359,15 +359,7 @@
             for i, block in enumerate((jnp.concatenate([t0[:4], t1[:4]], 0), jnp.concatenate([t0[4:], t1[4:]], 0))):
                 ZF[2 * j + i, h] = block
                 ZS[2 * j + i, h] = block.astype(bf16)
-        way = WAYS[h]
-        relay.append(send(ZS.at[at("z", 4), h], ZL.at[4, h], "z", way))
-        third.append({k: send(ZS.at[at("z", k), h], ZL.at[k, h], "z", k) for k in (-3 * way % Z, 2, 6)})
-
-    def pass_on(h):
-        k = 3 * WAYS[h] % Z
-        relay[h].wait_recv()
-        ZL[4, h] = (ZL[4, h].astype(f32) + ZF[at("z", k), h]).astype(bf16)
-        third[h].update({k: send(src, ZL.at[k, h], "z", k) for k, src in ((k, ZL.at[4, h]), (1, ZS.at[at("z", 1), h]), (7, ZS.at[at("z", 7), h]))})
+        third.append({k: send(ZS.at[at("z", k), h], ZL.at[k, h], "z", k) for k in far})
 
     begin_third(gate)
     end_first(up, u3)
@@ -376,10 +368,8 @@
     end_first(up, u0)
     for j in (u1, u3):
         third_down.update(end_down(j))
-    pass_on(gate)
     third_down.update(end_down(u0))
     begin_third(up)
-    pass_on(up)
     for copy in third_down.values():
         copy.wait_recv()
     real = lax.broadcasted_iota(jnp.int32, (24, 256), 0) < 22
@@ -434,7 +424,7 @@
         w = jnp.concatenate([jnp.where(odd, one[4:], one[:4]) for one in w], 0)
         m, v = (jnp.concatenate([IW[i, h, 0], IW[i, h, 1]], 0) for i in BOTH)
         WZ[z, h], *new = adamw(w, m, v, g_wide[h] * factor)
-        wide_z.append({k: send(WZ.at[z, h], WZ.at[z, h], "z", k) for k in (3, 5, 2, 6, 1, 7)})
+        wide_z.append({k: send(WZ.at[z, h], WZ.at[z, h], "z", k) for k in far})
         for i, one in enumerate(new):
             for layer in BOTH:
                 MW[i, h, layer] = one[4 * layer : 4 * layer + 4]
@@ -501,11 +491,6 @@
             arrive_pair(down[j], t)
             arrive_pair(down[j], t, True)
 
-    for h, way in enumerate(WAYS):
-        k = 3 * way % Z
-        wide_z[h].pop(k).wait_recv()
-        other = WZ.at[at("z", -k), h]
-        wide_z[h][4] = send(other, other, "z", way)
     begin_down(0)
     for h in BOTH:
         begin_wide(h)

time: 106 us -> 105 us (level)
  no operation moved by 1% of the time
where the time goes in v9:
time: 105 us; the launch traced here: 104 us
  Pallas kernels  103 us (98%)
    pallas_call x1, Pallas kernels, step_kernel(): pl.pallas_call(kernel, out_shape=(pltpu.VMEM((*pair, *square), bf16), plt...  99.4 us
    pallas_call x1, Pallas kernels, step_kernel(): pl.pallas_call(finish, out_shape=(shape((2, *square), bf16),) * 2 + (shap...  3.57 us

profile of v9, /device:TPU:2, one launch (start us, length us, event | category | flops | bytes accessed | tf_op | source)
XLA Modules:
  0.0 103.6 jit_solution(16784550998324626922)
XLA Ops:
  0.6 99.4 %clipped_step.1 = (bf16[2,2,4,4,32,1408]{5,4,3,2,1,0:T(8,128)(2,1)S(1)}, bf16[2,1408,512]{2,1,0:T(8,128)(2,1)S(1)}, f32[2,2,2,4,1408]{4,3,2,1,0:T(4,128)S(1)}, f32[2,11,2,512]{3,2,1,0:T(2,128)S(1)}) custom-call(bf16[704,704]{1,0:T(8,128)(2,1)} %constant.4.clone.pf, bf16[704,704]{1,0:T(8,128)(2,1)} %constant.5.clone.pb, bf16[2,4,4,32,1408]{4,3,2,1,0:T(8,128)(2,1)} %bitcast.9, ...), custom_call_target="tpu_custom_call" | custom-call | tf_op jit(solution)/shard_map/clipped_step/pallas_call | solution.py:565
  100.1 3.6 %finish.1 = (bf16[2,4,4,32,1408]{4,3,2,1,0:T(8,128)(2,1)}, bf16[2,4,4,32,1408]{4,3,2,1,0:T(8,128)(2,1)}, bf16[2,1408,512]{2,1,0:T(8,128)(2,1)}, f32[2,4,1408]{2,...) custom-call(bf16[2,2,4,4,32,1408]{5,4,3,2,1,0:T(8,128)(2,1)S(1)} %ge, ...), custom_call_target="tpu_custom_call" | custom-call | tf_op jit(solution)/shard_map/finish/pallas_call | solution.py:607

commit v10 on v9

--- a/solution.py
+++ b/solution.py
@@ -83,6 +83,11 @@
     def send_plane(i, source, target):
         ks = [k for k in (2, 1, 3, 0) if i or k]
         return {(i, k): send_to(at("x", i) * 32 + at("y", k) * 8 + z, source(k), target(k)) for k in ks}
+
+    def drain(count):
+        for copy in pending[:count]:
+            copy.wait_send()
+        del pending[:count]
 
     loads = {}
 
@@ -419,6 +424,7 @@
         copy.wait()
     odd = d % 2 == 1
     wide_z = []
+    scattered = len(pending)
     for h in BOTH:
         w = [OW[h, i].astype(f32) for i in BOTH]
         w = jnp.concatenate([jnp.where(odd, one[4:], one[:4]) for one in w], 0)
@@ -448,6 +454,7 @@
     spread_order = (0, 2, 1, 3)
     for i in spread_order:
         plane.update(send_plane(i, lambda k: mine, lambda k: mine))
+    drain(scattered)
     down = [Gather("z", functools.partial(lambda j, h, k: WD.at[h, at("z", k), at("x", j)], j)) for j in range(X)]
 
     def begin_down(j):
@@ -520,12 +527,14 @@
     arrive_wide(1, 1)
     both_down(2, 3)
     arrive_wide(3, 1)
+    early = len(pending)
     for j in spread_order[:2]:
         arrive_pair(down[j], 3)
     for h in BOTH:
         arrive_wide(2, h)
     for j in spread_order[2:]:
         arrive_pair(down[j], 3)
+    drain(early)
     loads["back", 0].wait()
     for j in spread_order:
         arrive_pair(down[j], 3, True)
@@ -541,8 +550,7 @@
             arrive_pair(wide[f][j], 1, True)
         for h in BOTH:
             arrive_wide(j, h, 2)
-    for copy in pending:
-        copy.wait_send()
+    drain(len(pending))
 
 
 def finish(W, OD, MW, MD, *rest):

time: 105 us -> 104 us (level)
  no operation moved by 1% of the time
where the time goes in v10:
time: 104 us; the launch traced here: 103 us
  Pallas kernels  103 us (99%)
    pallas_call x1, Pallas kernels, step_kernel(): pl.pallas_call(kernel, out_shape=(pltpu.VMEM((*pair, *square), bf16), plt...  99 us
    pallas_call x1, Pallas kernels, step_kernel(): pl.pallas_call(finish, out_shape=(shape((2, *square), bf16),) * 2 + (shap...  3.57 us

profile of v10, /device:TPU:2, one launch (start us, length us, event | category | flops | bytes accessed | tf_op | source)
XLA Modules:
  0.0 103.2 jit_solution(3228465292336146571)
XLA Ops:
  0.6 99.0 %clipped_step.1 = (bf16[2,2,4,4,32,1408]{5,4,3,2,1,0:T(8,128)(2,1)S(1)}, bf16[2,1408,512]{2,1,0:T(8,128)(2,1)S(1)}, f32[2,2,2,4,1408]{4,3,2,1,0:T(4,128)S(1)}, f32[2,11,2,512]{3,2,1,0:T(2,128)S(1)}) custom-call(bf16[704,704]{1,0:T(8,128)(2,1)} %constant.4.clone.pf, bf16[704,704]{1,0:T(8,128)(2,1)} %constant.5.clone.pb, bf16[2,4,4,32,1408]{4,3,2,1,0:T(8,128)(2,1)} %bitcast.9, ...), custom_call_target="tpu_custom_call" | custom-call | tf_op jit(solution)/shard_map/clipped_step/pallas_call | solution.py:573
  99.6 3.6 %finish.1 = (bf16[2,4,4,32,1408]{4,3,2,1,0:T(8,128)(2,1)}, bf16[2,4,4,32,1408]{4,3,2,1,0:T(8,128)(2,1)}, bf16[2,1408,512]{2,1,0:T(8,128)(2,1)}, f32[2,4,1408]{2,...) custom-call(bf16[2,2,4,4,32,1408]{5,4,3,2,1,0:T(8,128)(2,1)S(1)} %ge, ...), custom_call_target="tpu_custom_call" | custom-call | tf_op jit(solution)/shard_map/finish/pallas_call | solution.py:615
